TPU v7x, 32 devices: a whole 2x2x4 slice. The times are simulated.
32 devices in a mesh: dp: 16 (over z, y, x), mp: 2 (over core).
Axes of the slice: x: 2, y: 2, z: 4, core: 2. Of those that a mesh axis runs over, the one named last changes fastest.
Arguments:
- inputs: float32 [128, 197, 384], P('dp'), may hold values from -6 to 6
- cotangent: float32 [128, 197, 384], P('dp'), may hold values from -6 to 6
- first_gain: float32 [384], P('dp'), may hold values from 0.5 to 1.5
- first_shift: float32 [384], P('dp'), may hold values from -3 to 3
- mixer_weight: float32 [384, 3, 384], P('dp', None, 'mp'), may hold values from -6 to 6
- mixer_bias: float32 [2, 6, 64], P(None, 'mp', 'dp'), may hold values from -3 to 3
- output_weight: float32 [384, 384], P('mp', 'dp'), may hold values from -1.25 to 1.25
- output_bias: float32 [384], P('dp'), may hold values from -3 to 3
- second_gain: float32 [384], P('dp'), may hold values from 0.5 to 1.5
- second_shift: float32 [384], P('dp'), may hold values from -3 to 3
- expand_weight: float32 [384, 1536], P('dp', 'mp'), may hold values from -0.3125 to 0.3125
- expand_bias: float32 [24, 64], P('mp', 'dp'), may hold values from -3 to 3
- reduce_weight: float32 [1536, 384], P('mp', 'dp'), may hold values from -0.15625 to 0.15625
- reduce_bias: float32 [384], P('dp'), may hold values from -3 to 3
- momentum_first_gain: float32 [384], P('dp'), may hold values from -0.75 to 0.75
- momentum_first_shift: float32 [384], P('dp'), may hold values from -0.75 to 0.75
- momentum_mixer_weight: float32 [384, 3, 384], P('dp', None, 'mp'), may hold values from -0.75 to 0.75
- momentum_mixer_bias: float32 [2, 6, 64], P(None, 'mp', 'dp'), may hold values from -0.75 to 0.75
- momentum_output_weight: float32 [384, 384], P('mp', 'dp'), may hold values from -0.75 to 0.75
- momentum_output_bias: float32 [384], P('dp'), may hold values from -0.75 to 0.75
- momentum_second_gain: float32 [384], P('dp'), may hold values from -0.75 to 0.75
- momentum_second_shift: float32 [384], P('dp'), may hold values from -0.75 to 0.75
- momentum_expand_weight: float32 [384, 1536], P('dp', 'mp'), may hold values from -0.75 to 0.75
- momentum_expand_bias: float32 [24, 64], P('mp', 'dp'), may hold values from -0.75 to 0.75
- momentum_reduce_weight: float32 [1536, 384], P('mp', 'dp'), may hold values from -0.75 to 0.75
- momentum_reduce_bias: float32 [384], P('dp'), may hold values from -0.75 to 0.75
- variance_first_gain: float32 [384], P('dp'), may hold values from 0.0001 to 0.001
- variance_first_shift: float32 [384], P('dp'), may hold values from 0.0001 to 0.001
- variance_mixer_weight: float32 [384, 3, 384], P('dp', None, 'mp'), may hold values from 0.0001 to 0.001
- variance_mixer_bias: float32 [2, 6, 64], P(None, 'mp', 'dp'), may hold values from 0.0001 to 0.001
- variance_output_weight: float32 [384, 384], P('mp', 'dp'), may hold values from 0.0001 to 0.001
- variance_output_bias: float32 [384], P('dp'), may hold values from 0.0001 to 0.001
- variance_second_gain: float32 [384], P('dp'), may hold values from 0.0001 to 0.001
- variance_second_shift: float32 [384], P('dp'), may hold values from 0.0001 to 0.001
- variance_expand_weight: float32 [384, 1536], P('dp', 'mp'), may hold values from 0.0001 to 0.001
- variance_expand_bias: float32 [24, 64], P('mp', 'dp'), may hold values from 0.0001 to 0.001
- variance_reduce_weight: float32 [1536, 384], P('mp', 'dp'), may hold values from 0.0001 to 0.001
- variance_reduce_bias: float32 [384], P('dp'), may hold values from 0.0001 to 0.001
Outputs:
- block_out: float32 [128, 197, 384], P('dp')
- input_gradient: float32 [128, 197, 384], P('dp')
- gradient_first_gain: float32 [384], P('dp')
- gradient_first_shift: float32 [384], P('dp')
- gradient_mixer_weight: float32 [384, 3, 384], P('dp', None, 'mp')
- gradient_mixer_bias: float32 [2, 6, 64], P(None, 'mp', 'dp')
- gradient_output_weight: float32 [384, 384], P('mp', 'dp')
- gradient_output_bias: float32 [384], P('dp')
- gradient_second_gain: float32 [384], P('dp')
- gradient_second_shift: float32 [384], P('dp')
- gradient_expand_weight: float32 [384, 1536], P('dp', 'mp')
- gradient_expand_bias: float32 [24, 64], P('mp', 'dp')
- gradient_reduce_weight: float32 [1536, 384], P('mp', 'dp')
- gradient_reduce_bias: float32 [384], P('dp')
- updated_first_gain: float32 [384], P('dp')
- updated_first_shift: float32 [384], P('dp')
- updated_mixer_weight: float32 [384, 3, 384], P('dp', None, 'mp')
- updated_mixer_bias: float32 [2, 6, 64], P(None, 'mp', 'dp')
- updated_output_weight: float32 [384, 384], P('mp', 'dp')
- updated_output_bias: float32 [384], P('dp')
- updated_second_gain: float32 [384], P('dp')
- updated_second_shift: float32 [384], P('dp')
- updated_expand_weight: float32 [384, 1536], P('dp', 'mp')
- updated_expand_bias: float32 [24, 64], P('mp', 'dp')
- updated_reduce_weight: float32 [1536, 384], P('mp', 'dp')
- updated_reduce_bias: float32 [384], P('dp')
- updated_momentum_first_gain: float32 [384], P('dp')
- updated_momentum_first_shift: float32 [384], P('dp')
- updated_momentum_mixer_weight: float32 [384, 3, 384], P('dp', None, 'mp')
- updated_momentum_mixer_bias: float32 [2, 6, 64], P(None, 'mp', 'dp')
- updated_momentum_output_weight: float32 [384, 384], P('mp', 'dp')
- updated_momentum_output_bias: float32 [384], P('dp')
- updated_momentum_second_gain: float32 [384], P('dp')
- updated_momentum_second_shift: float32 [384], P('dp')
- updated_momentum_expand_weight: float32 [384, 1536], P('dp', 'mp')
- updated_momentum_expand_bias: float32 [24, 64], P('mp', 'dp')
- updated_momentum_reduce_weight: float32 [1536, 384], P('mp', 'dp')
- updated_momentum_reduce_bias: float32 [384], P('dp')
- updated_variance_first_gain: float32 [384], P('dp')
- updated_variance_first_shift: float32 [384], P('dp')
- updated_variance_mixer_weight: float32 [384, 3, 384], P('dp', None, 'mp')
- updated_variance_mixer_bias: float32 [2, 6, 64], P(None, 'mp', 'dp')
- updated_variance_output_weight: float32 [384, 384], P('mp', 'dp')
- updated_variance_output_bias: float32 [384], P('dp')
- updated_variance_second_gain: float32 [384], P('dp')
- updated_variance_second_shift: float32 [384], P('dp')
- updated_variance_expand_weight: float32 [384, 1536], P('dp', 'mp')
- updated_variance_expand_bias: float32 [24, 64], P('mp', 'dp')
- updated_variance_reduce_weight: float32 [1536, 384], P('mp', 'dp')
- updated_variance_reduce_bias: float32 [384], P('dp')
All inputs are finite; a program needn't handle non-finite values.
Results may differ from a plain program's by a relative error of at most 0.0003.
Values sent between devices are 32-bit elements; how exact they have to be, the bound alone decides.
A program may use at most 192 MiB of HBM per device.

v0:
```python
import jax
import jax.numpy as jnp
from jax import lax
from jax.sharding import PartitionSpec as P

HD = 64


norm_eps = 1e-06
beta_one = 0.9
beta_two = 0.99
adam_eps = 1e-08
learn_rate = 0.05
weight_decay = 0.05
step_count = 3.0
highest = lax.Precision.HIGHEST


def normalize(values):
    center = values - jnp.mean(values, axis=-1, keepdims=True)
    inverse = lax.rsqrt(jnp.mean(center * center, axis=-1, keepdims=True) + norm_eps)
    return (center * inverse, inverse)


def norm_backward(grad_out, normed, inverse, gain):
    grad_gain = jnp.sum(grad_out * normed, axis=(0, 1))
    grad_shift = jnp.sum(grad_out, axis=(0, 1))
    scaled = grad_out * gain
    grad_in = inverse * (
        scaled
        - jnp.mean(scaled, axis=-1, keepdims=True)
        - normed * jnp.mean(scaled * normed, axis=-1, keepdims=True)
    )
    return (grad_in, grad_gain, grad_shift)


def exact_gelu(values):
    return jax.nn.gelu(values, approximate=False)


def adam_update(param, grad, momentum, variance, decay):
    momentum_next = beta_one * momentum + (1.0 - beta_one) * grad
    variance_next = beta_two * variance + (1.0 - beta_two) * grad * grad
    mean_hat = momentum_next / (1.0 - beta_one**step_count)
    square_hat = variance_next / (1.0 - beta_two**step_count)
    stepped = param - learn_rate * (mean_hat / (jnp.sqrt(square_hat) + adam_eps) + decay * param)
    return (stepped, momentum_next, variance_next)


def per_device(
    inputs,
    cotangent,
    first_gain,
    first_shift,
    mixer_weight,
    mixer_bias,
    output_weight,
    output_bias,
    second_gain,
    second_shift,
    expand_weight,
    expand_bias,
    reduce_weight,
    reduce_bias,
    momentum_first_gain,
    momentum_first_shift,
    momentum_mixer_weight,
    momentum_mixer_bias,
    momentum_output_weight,
    momentum_output_bias,
    momentum_second_gain,
    momentum_second_shift,
    momentum_expand_weight,
    momentum_expand_bias,
    momentum_reduce_weight,
    momentum_reduce_bias,
    variance_first_gain,
    variance_first_shift,
    variance_mixer_weight,
    variance_mixer_bias,
    variance_output_weight,
    variance_output_bias,
    variance_second_gain,
    variance_second_shift,
    variance_expand_weight,
    variance_expand_bias,
    variance_reduce_weight,
    variance_reduce_bias,
):
    scale = (lax.axis_size("dp") * inputs.shape[0] * inputs.shape[1]) ** (-0.5)
    whole = (
        lax.all_gather(first_gain, "dp", axis=0, tiled=True),
        lax.all_gather(first_shift, "dp", axis=0, tiled=True),
        lax.all_gather(mixer_weight, "dp", axis=0, tiled=True),
        lax.all_gather(mixer_bias, "dp", axis=2, tiled=True),
        lax.all_gather(output_weight, "dp", axis=1, tiled=True),
        lax.all_gather(output_bias, "dp", axis=0, tiled=True),
        lax.all_gather(second_gain, "dp", axis=0, tiled=True),
        lax.all_gather(second_shift, "dp", axis=0, tiled=True),
        lax.all_gather(expand_weight, "dp", axis=0, tiled=True),
        lax.all_gather(expand_bias, "dp", axis=1, tiled=True),
        lax.all_gather(reduce_weight, "dp", axis=1, tiled=True),
        lax.all_gather(reduce_bias, "dp", axis=0, tiled=True),
    )
    (
        full_gain_one,
        full_shift_one,
        full_mixer,
        full_mixer_bias,
        full_output,
        full_output_bias,
        full_gain_two,
        full_shift_two,
        full_expand,
        full_expand_bias,
        full_reduce,
        full_reduce_bias,
    ) = whole
    images, length = (inputs.shape[0], inputs.shape[1])
    local_heads = full_mixer.shape[2] // HD
    width = local_heads * HD
    score_scale = HD ** (-0.5)
    first_normed, first_inverse = normalize(inputs)
    first_out = first_normed * full_gain_one + full_shift_one
    mixed = jnp.einsum("bsd,dcf->bscf", first_out, full_mixer, precision=highest)
    query = (mixed[:, :, 0] + full_mixer_bias[0].reshape(-1)).reshape(
        images, length, local_heads, HD
    )
    keys_local = mixed[:, :, 1].reshape(images, length, local_heads, HD)
    values = (mixed[:, :, 2] + full_mixer_bias[1].reshape(-1)).reshape(
        images, length, local_heads, HD
    )
    scores = jnp.einsum("bqhe,bkhe->bhqk", query, keys_local, precision=highest) * score_scale
    top = jnp.max(scores, axis=-1, keepdims=True)
    expon = jnp.exp(scores - top)
    total = jnp.sum(expon, axis=-1, keepdims=True)
    log_total = top + jnp.log(total)
    heads = jnp.einsum("bhqk,bkhe->bqhe", expon / total, values, precision=highest)
    heads_flat = heads.reshape(images, length, width)
    attention_part = jnp.einsum("bsf,fd->bsd", heads_flat, full_output, precision=highest)
    attention_whole = lax.psum(attention_part, "mp")
    middle = inputs + attention_whole + full_output_bias
    second_normed, second_inverse = normalize(middle)
    second_out = second_normed * full_gain_two + full_shift_two
    hidden = jnp.einsum(
        "bsd,df->bsf", second_out, full_expand, precision=highest
    ) + full_expand_bias.reshape(-1)
    active = exact_gelu(hidden)
    feed_part = jnp.einsum("bsf,fd->bsd", active, full_reduce, precision=highest)
    feed_whole = lax.psum(feed_part, "mp")
    block_out = middle + feed_whole + full_reduce_bias
    again = (
        lax.all_gather(first_gain, "dp", axis=0, tiled=True),
        lax.all_gather(first_shift, "dp", axis=0, tiled=True),
        lax.all_gather(mixer_weight, "dp", axis=0, tiled=True),
        lax.all_gather(mixer_bias, "dp", axis=2, tiled=True),
        lax.all_gather(output_weight, "dp", axis=1, tiled=True),
        lax.all_gather(output_bias, "dp", axis=0, tiled=True),
        lax.all_gather(second_gain, "dp", axis=0, tiled=True),
        lax.all_gather(second_shift, "dp", axis=0, tiled=True),
        lax.all_gather(expand_weight, "dp", axis=0, tiled=True),
        lax.all_gather(expand_bias, "dp", axis=1, tiled=True),
        lax.all_gather(reduce_weight, "dp", axis=1, tiled=True),
        lax.all_gather(reduce_bias, "dp", axis=0, tiled=True),
    )
    (
        back_gain_one,
        back_shift_one,
        back_mixer,
        back_mixer_bias,
        back_output,
        back_output_bias,
        back_gain_two,
        back_shift_two,
        back_expand,
        back_expand_bias,
        back_reduce,
        back_reduce_bias,
    ) = again
    grad_reduce_bias = jnp.sum(cotangent, axis=(0, 1)) * scale
    grad_reduce = jnp.einsum("bsf,bsd->fd", active, cotangent, precision=highest) * scale
    grad_active = jnp.einsum("bsd,fd->bsf", cotangent, back_reduce, precision=highest)
    grad_hidden = jax.vjp(exact_gelu, hidden)[1](grad_active)[0]
    grad_expand_bias = (jnp.sum(grad_hidden, axis=(0, 1)) * scale).reshape(-1, HD)
    grad_expand = jnp.einsum("bsd,bsf->df", second_out, grad_hidden, precision=highest) * scale
    second_part = jnp.einsum("bsf,df->bsd", grad_hidden, back_expand, precision=highest)
    grad_second_out = lax.psum(second_part, "mp")
    grad_norm_two, grad_gain_two, grad_shift_two = norm_backward(
        grad_second_out, second_normed, second_inverse, back_gain_two
    )
    grad_gain_two = grad_gain_two * scale
    grad_shift_two = grad_shift_two * scale
    grad_middle = cotangent + grad_norm_two
    grad_output_bias = jnp.sum(grad_middle, axis=(0, 1)) * scale
    grad_output = jnp.einsum("bsf,bsd->fd", heads_flat, grad_middle, precision=highest) * scale
    grad_heads = jnp.einsum("bsd,fd->bsf", grad_middle, back_output, precision=highest).reshape(
        images, length, local_heads, HD
    )
    again_scores = jnp.einsum("bqhe,bkhe->bhqk", query, keys_local, precision=highest) * score_scale
    probs = jnp.exp(again_scores - log_total)
    grad_values = jnp.einsum("bhqk,bqhe->bkhe", probs, grad_heads, precision=highest)
    grad_probs = jnp.einsum("bqhe,bkhe->bhqk", grad_heads, values, precision=highest)
    row_terms = jnp.transpose(jnp.sum(grad_heads * heads, axis=-1), (0, 2, 1))[..., None]
    grad_scores = probs * (grad_probs - row_terms) * score_scale
    grad_query = jnp.einsum("bhqk,bkhe->bqhe", grad_scores, keys_local, precision=highest)
    grad_keys = jnp.einsum("bhqk,bqhe->bkhe", grad_scores, query, precision=highest)
    grad_mixed = jnp.stack(
        [
            grad_query.reshape(images, length, width),
            grad_keys.reshape(images, length, width),
            grad_values.reshape(images, length, width),
        ],
        axis=2,
    )
    grad_mixer = jnp.einsum("bsd,bscf->dcf", first_out, grad_mixed, precision=highest) * scale
    grad_mixer_bias = (
        jnp.stack([jnp.sum(grad_query, axis=(0, 1)), jnp.sum(grad_values, axis=(0, 1))]) * scale
    )
    first_part = jnp.einsum("bscf,dcf->bsd", grad_mixed, back_mixer, precision=highest)
    grad_first_out = lax.psum(first_part, "mp")
    grad_norm_one, grad_gain_one, grad_shift_one = norm_backward(
        grad_first_out, first_normed, first_inverse, back_gain_one
    )
    grad_gain_one = grad_gain_one * scale
    grad_shift_one = grad_shift_one * scale
    input_gradient = grad_middle + grad_norm_one
    gradients = tuple(
        (
            lax.psum_scatter(grad_gain_one, "dp", scatter_dimension=0, tiled=True),
            lax.psum_scatter(grad_shift_one, "dp", scatter_dimension=0, tiled=True),
            lax.psum_scatter(grad_mixer, "dp", scatter_dimension=0, tiled=True),
            lax.psum_scatter(grad_mixer_bias, "dp", scatter_dimension=2, tiled=True),
            lax.psum_scatter(grad_output, "dp", scatter_dimension=1, tiled=True),
            lax.psum_scatter(grad_output_bias, "dp", scatter_dimension=0, tiled=True),
            lax.psum_scatter(grad_gain_two, "dp", scatter_dimension=0, tiled=True),
            lax.psum_scatter(grad_shift_two, "dp", scatter_dimension=0, tiled=True),
            lax.psum_scatter(grad_expand, "dp", scatter_dimension=0, tiled=True),
            lax.psum_scatter(grad_expand_bias, "dp", scatter_dimension=1, tiled=True),
            lax.psum_scatter(grad_reduce, "dp", scatter_dimension=1, tiled=True),
            lax.psum_scatter(grad_reduce_bias, "dp", scatter_dimension=0, tiled=True),
        )
    )
    params = (
        first_gain,
        first_shift,
        mixer_weight,
        mixer_bias,
        output_weight,
        output_bias,
        second_gain,
        second_shift,
        expand_weight,
        expand_bias,
        reduce_weight,
        reduce_bias,
    )
    momenta = (
        momentum_first_gain,
        momentum_first_shift,
        momentum_mixer_weight,
        momentum_mixer_bias,
        momentum_output_weight,
        momentum_output_bias,
        momentum_second_gain,
        momentum_second_shift,
        momentum_expand_weight,
        momentum_expand_bias,
        momentum_reduce_weight,
        momentum_reduce_bias,
    )
    variances = (
        variance_first_gain,
        variance_first_shift,
        variance_mixer_weight,
        variance_mixer_bias,
        variance_output_weight,
        variance_output_bias,
        variance_second_gain,
        variance_second_shift,
        variance_expand_weight,
        variance_expand_bias,
        variance_reduce_weight,
        variance_reduce_bias,
    )
    decays = (
        0.0,
        0.0,
        weight_decay,
        0.0,
        weight_decay,
        0.0,
        0.0,
        0.0,
        weight_decay,
        0.0,
        weight_decay,
        0.0,
    )
    results = [
        adam_update(p, g, m, v, w)
        for p, g, m, v, w in zip(params, gradients, momenta, variances, decays)
    ]
    stepped = tuple((item[0] for item in results))
    moments = tuple((item[1] for item in results))
    squares = tuple((item[2] for item in results))
    return (block_out, input_gradient, *gradients, *stepped, *moments, *squares)


def solution(mesh):
    return jax.shard_map(
        per_device,
        mesh=mesh,
        in_specs=(
            P("dp", None, None),
            P("dp", None, None),
            P("dp"),
            P("dp"),
            P("dp", None, "mp"),
            P(None, "mp", "dp"),
            P("mp", "dp"),
            P("dp"),
            P("dp"),
            P("dp"),
            P("dp", "mp"),
            P("mp", "dp"),
            P("mp", "dp"),
            P("dp"),
            P("dp"),
            P("dp"),
            P("dp", None, "mp"),
            P(None, "mp", "dp"),
            P("mp", "dp"),
            P("dp"),
            P("dp"),
            P("dp"),
            P("dp", "mp"),
            P("mp", "dp"),
            P("mp", "dp"),
            P("dp"),
            P("dp"),
            P("dp"),
            P("dp", None, "mp"),
            P(None, "mp", "dp"),
            P("mp", "dp"),
            P("dp"),
            P("dp"),
            P("dp"),
            P("dp", "mp"),
            P("mp", "dp"),
            P("mp", "dp"),
            P("dp"),
        ),
        out_specs=(
            P("dp", None, None),
            P("dp", None, None),
            P("dp"),
            P("dp"),
            P("dp", None, "mp"),
            P(None, "mp", "dp"),
            P("mp", "dp"),
            P("dp"),
            P("dp"),
            P("dp"),
            P("dp", "mp"),
            P("mp", "dp"),
            P("mp", "dp"),
            P("dp"),
            P("dp"),
            P("dp"),
            P("dp", None, "mp"),
            P(None, "mp", "dp"),
            P("mp", "dp"),
            P("dp"),
            P("dp"),
            P("dp"),
            P("dp", "mp"),
            P("mp", "dp"),
            P("mp", "dp"),
            P("dp"),
            P("dp"),
            P("dp"),
            P("dp", None, "mp"),
            P(None, "mp", "dp"),
            P("mp", "dp"),
            P("dp"),
            P("dp"),
            P("dp"),
            P("dp", "mp"),
            P("mp", "dp"),
            P("mp", "dp"),
            P("dp"),
            P("dp"),
            P("dp"),
            P("dp", None, "mp"),
            P(None, "mp", "dp"),
            P("mp", "dp"),
            P("dp"),
            P("dp"),
            P("dp"),
            P("dp", "mp"),
            P("mp", "dp"),
            P("mp", "dp"),
            P("dp"),
        ),
        check_vma=False,
    )
```

profile of v0, /device:TPU:0, one launch (start us, length us, event | category | flops | bytes accessed | tf_op | source)
XLA Modules:
  0.0 1011.6 jit_solution(15945376760257392558)
XLA Ops:
  8.1 0.9 copy.229
  9.1 42.7 %all_gather.45 = f32[2,3,64]{1,0,2:T(2,128)S(1)} all-gather(f32[2,3,4]{1,0,2:T(2,128)S(1)} %copy.229), channel_id=1, replica_groups=mesh['dp'=16,'mp'=2] {'dp'}, dimensions={2}, use_global_device_ids=true | all-gather | bytes 1632 | tf_op jit(solution)/shard_map/all_gather | solution.py:95
  52.0 2.0 reduce_sum.171
  54.2 0.9 multiply_reduce_fusion.6
  55.1 37.6 %all_gather.46 = f32[192,384]{0,1:T(8,128)S(1)} all-gather(f32[192,24]{0,1:T(8,128)S(1)} %copy-done.28), channel_id=1, replica_groups=mesh['dp'=16,'mp'=2] {'dp'}, dimensions={1}, use_global_device_ids=true | all-gather | bytes 313344 | tf_op jit(solution)/shard_map/all_gather | solution.py:96
  92.7 48.5 %all_gather.44 = f32[384,3,192]{2,0,1:T(8,128)} all-gather(f32[24,3,192]{2,0,1:T(8,128)S(1)} %copy-done.25), channel_id=1, replica_groups=mesh['dp'=16,'mp'=2] {'dp'}, dimensions={0}, use_global_device_ids=true | all-gather | bytes 940032 | tf_op jit(solution)/shard_map/all_gather | solution.py:94
  143.7 71.9 %all-reduce.15 = (f32[384]{0:T(512)S(1)}, f32[384]{0:T(512)S(1)}, f32[384]{0:T(512)S(1)}, f32[384]{0:T(512)S(1)}, f32[384]{0:T(512)S(1)}) all-reduce(f32[384]{0:T(512)S(1)} %dynamic-update-slice.1, f32[384]{0:T(512)S(1)} %dynamic-update-slice, f32[384]{0:T(512)S(1)} %dynamic-update-slice.2, ...), channel_id=1, replica_groups=mesh['dp'=16,'mp'=2] {'dp'}, use_global_device_ids=true, to_apply=%add.1 | all-reduce | flops 1920 | bytes 15360
  215.6 9.9 fusion.15
  226.0 5.0 multiply_reduce_fusion
  231.0 0.9 fusion.8
  231.9 1.2 copy-done.1
  233.1 4.2 fusion.6
  237.3 1.1 copy-done.13
  238.5 7.8 fusion.81
  247.5 36.2 %all-gather = f32[16,4,12]{2,1,0:T(4,128)S(1)} all-gather(f32[1,4,12]{2,1,0:T(4,128)S(1)} %bitcast.140), channel_id=1, replica_groups=mesh['dp'=16,'mp'=2] {'dp'}, dimensions={0}, use_global_device_ids=true | all-gather | bytes 3264 | tf_op jit(solution)/shard_map/all_gather | solution.py:101
  283.9 2.5 fusion.118
  286.4 1.5 copy-done.2
  287.8 0.6 multiply_reduce_fusion.5
  288.5 12.8 %all-gather.4.cloned.1.call-done = f32[384,768]{1,0:T(8,128)} async-done(((f32[24,768]{1,0:T(8,128)}), f32[384,768]{1,0:T(8,128)}) %all-gather.4.cloned.1.call-update) | async-done | bytes 1179664 | tf_op jit(solution)/shard_map/all_gather | solution.py:100
  301.3 11.7 %fusion.64 = (u8[197,768]{1,0:T(8,128)(4,1)S(1)}, u8[197,768]{1,0:T(8,128)(4,1)S(1)}, f32[8,197,768]{2,1,0:T(8,128)S(1)}) fusion(f32[768]{0:T(1024)S(1)} %add.306, f32[384,768]{1,0:T(8,128)} %all-gather.4.cloned.1.call-done, f32[8,197,384]{2,1,0:T(8,128)} %copy-done.2, f32[384]{0:T(512)S(1)} %get-tuple-element.322, f32[384]{0:T(512)S(1)} %get-tuple-element.323, ...), kind=kOutput, calls=%fused_computation.95 | convolution fusion | flops 5596439040 | bytes 8763200 | tf_op jit(solution)/shard_map/bsd,df->bsf/dot_general | solution.py:145
  313.0 2.3 copy-done.4
  315.2 11.8 %fusion = f32[8,197,768]{2,1,0:T(8,128)} fusion(f32[8,197,768]{2,1,0:T(8,128)S(1)} %get-tuple-element.382, f32[768]{0:T(1024)S(1)} %add.306, u8[197,768]{1,0:T(8,128)(4,1)S(1)} %get-tuple-element.303, u8[197,768]{1,0:T(8,128)(4,1)S(1)} %get-tuple-element.302), kind=kLoop, calls=%fused_computation.1 | loop fusion | flops 82305024 | bytes 9988608 | tf_op jit(solution)/shard_map/erfc | solution.py:38
  327.0 31.6 %all-gather.6.cloned.1.call-done = f32[768,384]{0,1:T(8,128)} async-done(((f32[768,24]{0,1:T(8,128)}), f32[768,384]{0,1:T(8,128)}) %all-gather.6.cloned.1.call-update) | async-done | bytes 1179664 | tf_op jit(solution)/shard_map/all_gather | solution.py:102
  358.6 14.4 %fusion.122 = (f32[768]{0:T(1024)S(1)}, f32[8,197,768]{2,1,0:T(8,128)S(1)}) fusion(f32[8,197,768]{2,1,0:T(8,128)} %fusion, f32[768,384]{0,1:T(8,128)} %all-gather.6.cloned.1.call-done, f32[8,197,384]{2,0,1:T(8,128)} %param.39, f32[8,197,768]{2,1,0:T(8,128)} %copy-done.4, f32[768]{0:T(1024)S(1)} %add.306), kind=kOutput, calls=%fused_computation.196 | convolution fusion | flops 5595530240 | bytes 18130944 | tf_op jit(solution)/shard_map/bsd,fd->bsf/dot_general | solution.py:182
  373.1 2.2 copy-done.16
  375.2 9.4 fusion.68
  384.9 13.0 %fusion.42 = f32[768,384]{0,1:T(8,128)} fusion(f32[8,197,384]{2,0,1:T(8,128)} %param.39, f32[8,197,768]{2,1,0:T(8,128)} %fusion, f32[8,197,768]{2,1,0:T(8,128)} %copy-done.4, f32[768]{0:T(1024)S(1)} %add.306), kind=kOutput, calls=%fused_computation.79 | convolution fusion | flops 5581301760 | bytes 13286400 | tf_op jit(solution)/shard_map/bsf,bsd->fd/dot_general | solution.py:181
  398.5 11.9 %fusion.38 = f32[384,768]{1,0:T(8,128)} fusion(f32[8,197,768]{2,1,0:T(8,128)} %copy-done.16, f32[8,197,384]{2,1,0:T(8,128)} %copy-done.2, f32[384]{0:T(512)S(1)} %get-tuple-element.322, f32[384]{0:T(512)S(1)} %get-tuple-element.323, f32[8,197]{1,0:T(8,128)S(1)} %add_rsqrt_fusion, f32[8,197]{1,0:T(8,128)S(1)} %broadcast_multiply_fusion.4), kind=kOutput, calls=%fused_computation.77 | convolution fusion | flops 5580091392 | bytes 8457536 | tf_op jit(solution)/shard_map/bsd,bsf->df/dot_general | solution.py:185
  410.5 3.4 multiply_reduce_fusion.1
  414.4 2.7 fusion.117
  417.2 2.9 fusion.79
  420.1 1.1 copy-done.7
  421.6 5.9 fusion.65
  427.5 9.3 multiply_multiply_fusion
  436.8 6.1 fusion.31
  442.9 6.5 bitcast_reduce_fusion
  450.0 6.5 bitcast_reduce_fusion.1
  456.5 1.1 copy-done.22
  457.6 16.8 %fusion.48 = f32[384,3,192]{2,0,1:T(8,128)} fusion(f32[8,197,1,192]{1,3,2,0:T(8,128)S(1)} %bitcast.129, f32[8,197,1,192]{1,3,2,0:T(8,128)S(1)} %bitcast.127, f32[8,197,1,192]{1,3,2,0:T(8,128)S(1)} %bitcast.131, f32[384]{0:T(512)S(1)} %get-tuple-element.319, f32[384]{0:T(512)S(1)} %get-tuple-element.320, f32[8,197,384]{2,0,1:T(8,128)S(1)} %copy-done, ...), kind=kOutput, calls=%fused_computation.81 | convolution fusion | flops 4187489280 | bytes 6952256 | tf_op jit(solution)/shard_map/bsd,bscf->dcf/dot_general | solution.py:215
  474.5 12.4 %fusion.29 = f32[8,197,384]{2,1,0:T(8,128)} fusion(f32[8,197,768]{2,1,0:T(8,128)} %fusion, f32[8,197,768]{2,1,0:T(8,128)} %copy-done.4, f32[768]{0:T(1024)S(1)} %add.306, f32[768,384]{0,1:T(8,128)} %all-gather.6.cloned.1.call-done), kind=kOutput, calls=%fused_computation.65 | convolution fusion | flops 5581006848 | bytes 13286400 | tf_op jit(solution)/shard_map/bsf,fd->bsd/dot_general | solution.py:149
  487.0 20.0 %fusion.28 = f32[8,197,384]{2,1,0:T(8,128)} fusion(f32[8,197,1,192]{1,3,2,0:T(8,128)S(1)} %bitcast.130, f32[8,197,1,192]{1,3,2,0:T(8,128)S(1)} %bitcast.128, f32[8,197,1,192]{1,3,2,0:T(8,128)S(1)} %bitcast.132, f32[384,3,192]{2,0,1:T(8,128)S(1)} %copy-done.17), kind=kOutput, calls=%fused_computation.64 | convolution fusion | flops 4184847360 | bytes 6936576 | tf_op jit(solution)/shard_map/bscf,dcf->bsd/dot_general | solution.py:219
  508.6 1.9 reduce_sum.189
  510.9 10.9 %reduce-scatter.13.cloned.1.call-done = f32[768,24]{0,1:T(8,128)} async-done(((f32[768,384]{0,1:T(8,128)}), f32[768,24]{0,1:T(8,128)}) %reduce-scatter.13.cloned.1.call-update) | async-done | bytes 73744 | tf_op jit(solution)/shard_map/reduce_scatter | solution.py:239
  521.8 1.6 multiply_subtract_fusion
  523.4 127.8 %reduce-scatter.11.cloned.1.call-done = f32[24,768]{1,0:T(8,128)} async-done(((f32[384,768]{1,0:T(8,128)}), f32[24,768]{1,0:T(8,128)}) %reduce-scatter.11.cloned.1.call-update) | async-done | bytes 73744 | tf_op jit(solution)/shard_map/reduce_scatter | solution.py:237
  651.2 1.6 multiply_subtract_fusion.1
  652.8 125.9 %reduce-scatter.9.cloned.1.call-done = f32[192,24]{0,1:T(8,128)} async-done(((f32[192,384]{0,1:T(8,128)}), f32[192,24]{0,1:T(8,128)}) %reduce-scatter.9.cloned.1.call-update) | async-done | bytes 18448 | tf_op jit(solution)/shard_map/reduce_scatter | solution.py:233
  778.7 1.4 multiply_subtract_fusion.3
  780.0 128.0 %reduce-scatter.7.cloned.1.call-done = f32[24,3,192]{2,0,1:T(8,128)} async-done(((f32[384,3,192]{2,0,1:T(8,128)}), f32[24,3,192]{2,0,1:T(8,128)}) %reduce-scatter.7.cloned.1.call-update) | async-done | bytes 55312 | tf_op jit(solution)/shard_map/reduce_scatter | solution.py:231
  908.1 1.6 multiply_subtract_fusion.2
  909.7 3.1 multiply_reduce_fusion.2
  912.8 74.9 %all-reduce.14 = (f32[384]{0:T(512)S(1)}, f32[384]{0:T(512)S(1)}, f32[384]{0:T(512)S(1)}, f32[2,3,64]{2,1,0:T(4,128)S(1)}, f32[384]{0:T(512)S(1)}, /*index=5*/f3...) all-reduce(f32[384]{0:T(512)S(1)} %dynamic-update-slice.5, ...), channel_id=1, replica_groups=mesh['dp'=16,'mp'=2] {'dp'}, use_global_device_ids=true, to_apply=%add.5 | all-reduce | flops 3840 | bytes 30720
  987.7 2.7 add_add_fusion
  990.4 1.9 copy.253
  992.4 3.0 multiply_add_fusion.1
  995.6 1.9 copy.254
  997.6 0.6 copy.257
  999.9 0.6 multiply_subtract_fusion.10
  1000.5 0.6 multiply_subtract_fusion.9
  1001.2 0.6 multiply_subtract_fusion.8
  1001.8 0.6 multiply_subtract_fusion.7
  1002.4 0.6 multiply_subtract_fusion.6
  1003.0 0.6 multiply_subtract_fusion.5
  1003.6 0.6 multiply_subtract_fusion.4
  (188 shorter events, 8.8 us)
Async XLA Ops:
  8.1 46.1 %copy-start = (f32[8,197,384]{2,0,1:T(8,128)S(1)}, f32[8,197,384]{2,0,1:T(8,128)}, u32[]{:S(2)}) copy-start(f32[8,197,384]{2,0,1:T(8,128)} %param.38) | copy-start | bytes 7262212
  8.1 275.8 %all-reduce.21.cloned.1.call-start = ((), (), s32[]{:S(2)}) async-start(), calls=%async_computation.4 | async-start | bytes 4915200 | tf_op jit(solution)/shard_map/psum | solution.py:141
  52.0 3.1 copy-start.28
  52.0 40.7 %copy-start.25 = (f32[24,3,192]{2,0,1:T(8,128)S(1)}, f32[24,3,192]{2,0,1:T(8,128)}, u32[]{:S(2)}) copy-start(f32[24,3,192]{2,0,1:T(8,128)} %param.42) | copy-start | bytes 165892
  54.0 87.2 %copy-start.44 = (u32[32]{0:T(128)S(1)}, u32[32]{0:T(128)}, u32[]{:S(2)}) copy-start(u32[32]{0:T(128)} %constant.218) | copy-start | bytes 388
  54.1 88.4 %copy-start.54 = (f32[24]{0:T(128)S(1)}, f32[24]{0:T(128)}, u32[]{:S(2)}) copy-start(f32[24]{0:T(128)} %param.46) | copy-start | bytes 292
  54.1 88.7 %copy-start.57 = (f32[24]{0:T(128)S(1)}, f32[24]{0:T(128)}, u32[]{:S(2)}) copy-start(f32[24]{0:T(128)} %param.47) | copy-start | bytes 292
  54.1 88.9 %copy-start.51 = (f32[24]{0:T(128)S(1)}, f32[24]{0:T(128)}, u32[]{:S(2)}) copy-start(f32[24]{0:T(128)} %param.45) | copy-start | bytes 292
  54.1 89.1 %copy-start.45 = (f32[24]{0:T(128)S(1)}, f32[24]{0:T(128)}, u32[]{:S(2)}) copy-start(f32[24]{0:T(128)} %param.40) | copy-start | bytes 292
  54.1 89.3 %copy-start.48 = (f32[24]{0:T(128)S(1)}, f32[24]{0:T(128)}, u32[]{:S(2)}) copy-start(f32[24]{0:T(128)} %param.41) | copy-start | bytes 292
  225.9 5.0 copy-start.10
  225.9 5.0 copy-start.11
  226.0 5.9 copy-start.15
  238.5 9.0 copy-start.38
  246.3 55.0 %all-gather.4.cloned.1.call-start = ((), (), s32[]{:S(2)}) async-start(), calls=%async_computation.5 | async-start | bytes 1253376 | tf_op jit(solution)/shard_map/all_gather | solution.py:100
  246.9 111.8 %all-gather.6.cloned.1.call-start = ((), (), s32[]{:S(2)}) async-start(), calls=%async_computation.6 | async-start | bytes 1253376 | tf_op jit(solution)/shard_map/all_gather | solution.py:102
  247.4 163.0 %all-reduce.23.cloned.1.call-start = ((), (), s32[]{:S(2)}) async-start(), calls=%async_computation.7 | async-start | bytes 4915200 | tf_op jit(solution)/shard_map/psum | solution.py:187
  358.6 16.6 %copy-start.24 = (f32[384,768]{1,0:T(8,128)S(1)}, f32[384,768]{1,0:T(8,128)}, u32[]{:S(2)}) copy-start(f32[384,768]{1,0:T(8,128)} %all-gather.4.cloned.1.call-done) | copy-start | bytes 3538948
  384.6 137.2 %reduce-scatter.13.cloned.1.call-start = ((), (), s32[]{:S(2)}) async-start(), calls=%async_computation.11 | async-start | bytes 1253376 | tf_op jit(solution)/shard_map/reduce_scatter | solution.py:239
  397.9 253.2 %reduce-scatter.11.cloned.1.call-start = ((), (), s32[]{:S(2)}) async-start(), calls=%async_computation.10 | async-start | bytes 1253376 | tf_op jit(solution)/shard_map/reduce_scatter | solution.py:237
  410.4 368.3 %reduce-scatter.9.cloned.1.call-start = ((), (), s32[]{:S(2)}) async-start(), calls=%async_computation.9 | async-start | bytes 417792 | tf_op jit(solution)/shard_map/reduce_scatter | solution.py:233
  410.4 3.5 copy-start.3
  410.4 3.9 copy-start.9
  417.1 4.4 copy-start.6
  417.1 4.1 copy-start.14
  421.6 21.3 %slice-start = ((s8[4915200]{0:T(1024)(128)(4,1)}), s8[720896]{0:T(1024)(128)(4,1)S(1)}, s32[]{:S(2)}) async-start(s8[4915200]{0:T(1024)(128)(4,1)} %bitcast.114), calls=%async_computation.13 | async-start | bytes 1441792
  427.5 9.3 copy-start.12
  427.5 15.4 %slice-start.1 = ((s8[4915200]{0:T(1024)(128)(4,1)}), s8[4194304]{0:T(1024)(128)(4,1)S(1)}, s32[]{:S(2)}) async-start(s8[4915200]{0:T(1024)(128)(4,1)} %bitcast.114), calls=%async_computation.14 | async-start | bytes 8388608
  436.8 6.1 copy-start.5
  436.8 6.1 copy-start.8
  449.5 458.6 %reduce-scatter.7.cloned.1.call-start = ((), (), s32[]{:S(2)}) async-start(), calls=%async_computation.8 | async-start | bytes 1253376 | tf_op jit(solution)/shard_map/reduce_scatter | solution.py:231
  449.9 7.7 copy-start.18
  449.9 7.7 copy-start.20
  474.4 435.3 %all-reduce.25.cloned.1.call-start = ((), (), s32[]{:S(2)}) async-start(), calls=%async_computation.12 | async-start | bytes 9830400 | tf_op jit(solution)/shard_map/psum | solution.py:150
  474.5 12.5 %copy-start.17 = (f32[384,3,192]{2,0,1:T(8,128)S(1)}, f32[384,3,192]{2,0,1:T(8,128)}, u32[]{:S(2)}) copy-start(f32[384,3,192]{2,0,1:T(8,128)} %all_gather.44) | copy-start | bytes 2654212
  474.5 12.5 %copy-start.19 = (f32[8,3,64,197]{3,2,1,0:T(8,128)S(1)}, f32[8,3,64,197]{3,2,1,0:T(8,128)}, u32[]{:S(2)}) copy-start(f32[8,3,64,197]{3,2,1,0:T(8,128)} %fusion.31) | copy-start | bytes 3631108
  474.5 12.5 %copy-start.21 = (f32[8,3,64,197]{3,2,1,0:T(8,128)S(1)}, f32[8,3,64,197]{3,2,1,0:T(8,128)}, u32[]{:S(2)}) copy-start(f32[8,3,64,197]{3,2,1,0:T(8,128)} %get-tuple-element.384) | copy-start | bytes 3631108
  474.5 12.5 %copy-start.23 = (f32[8,3,64,197]{3,2,1,0:T(8,128)S(1)}, f32[8,3,64,197]{3,2,1,0:T(8,128)}, u32[]{:S(2)}) copy-start(f32[8,3,64,197]{3,2,1,0:T(8,128)} %copy-done.22) | copy-start | bytes 3631108
  507.0 3.5 copy-start.60
  507.0 14.8 %copy-start.26 = (f32[768,24]{0,1:T(8,128)S(1)}, f32[768,24]{0,1:T(8,128)}, u32[]{:S(2)}) copy-start(f32[768,24]{0,1:T(8,128)} %param.50) | copy-start | bytes 221188
  507.0 14.8 %copy-start.29 = (f32[768,24]{0,1:T(8,128)S(1)}, f32[768,24]{0,1:T(8,128)}, u32[]{:S(2)}) copy-start(f32[768,24]{0,1:T(8,128)} %param.62) | copy-start | bytes 221188
  507.1 14.7 %copy-start.30 = (f32[768,24]{0,1:T(8,128)S(1)}, f32[768,24]{0,1:T(8,128)}, u32[]{:S(2)}) copy-start(f32[768,24]{0,1:T(8,128)} %param.74) | copy-start | bytes 221188
  507.1 144.1 %copy-start.27 = (f32[24,768]{1,0:T(8,128)S(1)}, f32[24,768]{1,0:T(8,128)}, u32[]{:S(2)}) copy-start(f32[24,768]{1,0:T(8,128)} %param.48) | copy-start | bytes 221188
  507.1 144.1 %copy-start.31 = (f32[24,768]{1,0:T(8,128)S(1)}, f32[24,768]{1,0:T(8,128)}, u32[]{:S(2)}) copy-start(f32[24,768]{1,0:T(8,128)} %param.60) | copy-start | bytes 221188
  507.1 144.1 %copy-start.32 = (f32[24,768]{1,0:T(8,128)S(1)}, f32[24,768]{1,0:T(8,128)}, u32[]{:S(2)}) copy-start(f32[24,768]{1,0:T(8,128)} %param.72) | copy-start | bytes 221188
  507.1 271.6 %copy-start.35 = (f32[192,24]{0,1:T(8,128)S(1)}, f32[192,24]{0,1:T(8,128)}, u32[]{:S(2)}) copy-start(f32[192,24]{0,1:T(8,128)} %param.56) | copy-start | bytes 55300
  507.1 271.6 %copy-start.36 = (f32[192,24]{0,1:T(8,128)S(1)}, f32[192,24]{0,1:T(8,128)}, u32[]{:S(2)}) copy-start(f32[192,24]{0,1:T(8,128)} %param.68) | copy-start | bytes 55300
  507.1 400.9 %copy-start.33 = (f32[24,3,192]{2,0,1:T(8,128)S(1)}, f32[24,3,192]{2,0,1:T(8,128)}, u32[]{:S(2)}) copy-start(f32[24,3,192]{2,0,1:T(8,128)} %param.54) | copy-start | bytes 165892
  507.1 400.9 %copy-start.34 = (f32[24,3,192]{2,0,1:T(8,128)S(1)}, f32[24,3,192]{2,0,1:T(8,128)}, u32[]{:S(2)}) copy-start(f32[24,3,192]{2,0,1:T(8,128)} %param.66) | copy-start | bytes 165892
  992.4 11.2 %copy-start.39 = (f32[12,4]{0,1:T(4,128)}, f32[12,4]{0,1:T(4,128)S(1)}, u32[]{:S(2)}) copy-start(f32[12,4]{0,1:T(4,128)S(1)} %copy.256) | copy-start | bytes 580
  995.5 4.5 copy-start.46
  995.5 4.5 copy-start.47
  995.5 5.1 copy-start.49
  995.5 5.0 copy-start.50
  995.5 5.6 copy-start.52
  995.5 5.6 copy-start.53
  995.5 6.2 copy-start.55
  995.6 6.2 copy-start.56
  995.6 6.8 copy-start.58
  995.6 6.8 copy-start.59
  995.6 7.4 copy-start.61
  995.6 7.4 copy-start.62
  995.6 8.0 copy-start.42
  995.6 8.0 copy-start.43
  (10 other events, 17.8 us)
Sparse Core Ops, SparseCore 0:
  246.4 17.7 all-reduce.20
  384.8 20.7 all-reduce.22
  507.1 27.6 all-reduce.24
Sparse Core Ops, SparseCore 1:
  249.6 51.7 all-gather.3
  304.0 54.6 all-gather.5
  398.0 123.7 reduce-scatter.12
  527.1 124.0 reduce-scatter.10
  656.4 122.2 reduce-scatter.8
  784.0 124.0 reduce-scatter.6
where the time goes:
time: 1020 us; the launch traced here: 1010 us
  waiting for transfers between devices  438 us (43%)
  blocking collectives  312 us (31%)
  matrix products  174 us (17%)
  other arithmetic  46.6 us (5%)
  local copies, waits for them, and re-layouts  21.4 us (2%)
  between operations  18.6 us (2%)
    unnamed x2, blocking collectives  147 us
    reduce_scatter x1, waiting for transfers between devices, per_device(): lax.psum_scatter(grad_mixer, 'dp', scatter_dimension=0, tiled=True)  128 us
    reduce_scatter x1, waiting for transfers between devices, per_device(): lax.psum_scatter(grad_expand, 'dp', scatter_dimension=0, tiled=True)  128 us
    reduce_scatter x1, waiting for transfers between devices, per_device(): lax.psum_scatter(grad_output, 'dp', scatter_dimension=1, tiled=True)  126 us
    all_gather x1, blocking collectives, per_device(): lax.all_gather(mixer_weight, 'dp', axis=0, tiled=True)  48.5 us
    all_gather x1, blocking collectives, per_device(): lax.all_gather(mixer_bias, 'dp', axis=2, tiled=True)  42.7 us
    all_gather x1, blocking collectives, per_device(): lax.all_gather(output_weight, 'dp', axis=1, tiled=True)  37.6 us
    all_gather x1, blocking collectives, per_device(): lax.all_gather(expand_bias, 'dp', axis=1, tiled=True)  36.2 us
  transfers between devices with their start and end apart: 9, of which 6 were waited for; matrix products, arithmetic and copies ran while one was open for 15% of the time, Pallas kernels for 0%

commit v1 on v0

v1 whole, which is shorter than its diff:
```python
import functools
import heapq

import jax
import jax.numpy as jnp
from jax import lax
from jax.experimental import pallas as pl
from jax.experimental.pallas import tpu as pltpu
from jax.sharding import PartitionSpec as P

norm_eps = 1e-06
beta_one = 0.9
beta_two = 0.99
adam_eps = 1e-08
learn_rate = 0.05
weight_decay = 0.05
step_count = 3.0

LANES = 128
MASKED = -1e30
f32, bf16 = jnp.float32, jnp.bfloat16


def split(x):
    high = x.astype(bf16)
    return high, (x - high.astype(f32)).astype(bf16)


def dot(a, b, da, db):
    return lax.dot_general(a, b, (((da,), (db,)), ((), ())), preferred_element_type=f32)


def product(a, b, da, db):
    left = jnp.concatenate([a[0], a[0], a[1]], axis=da)
    right = jnp.concatenate([b[0], b[1], b[0]], axis=db)
    return dot(left, right, da, db)


def product_apart(a, b, da, db):
    return dot(a[0], b[0], da, db) + dot(a[0], b[1], da, db) + dot(a[1], b[0], da, db)


def layer_kernel(length, heads, head, base, x_ref, cot_ref, w_ref, vec_ref, mb_ref, eb_ref,
                 y_ref, gx_ref, g_ref, sg_ref,
                 whi, wlo, wsem, pad, mixed, probs_hi, probs_lo, joined,
                 fo_hi, fo_lo, so_hi, so_lo, cot_hi, cot_lo, gm_hi, gm_lo, part, part2):
    step = pl.program_id(0)
    rows, width = pad.shape[1], pad.shape[2]
    local = heads * head
    qkv = 5 * LANES
    hidden_local = eb_ref.shape[-1]
    attn = 6 * LANES
    up, down, end = attn, attn + hidden_local, attn + 2 * hidden_local

    @pl.when(step == 0)
    def _():
        for c in range(2):
            pltpu.make_async_copy(w_ref.at[c], g_ref.at[c], wsem.at[c]).start()
        pad[...] = jnp.zeros_like(pad)
        sg_ref[...] = jnp.zeros_like(sg_ref)
        for c in range(2):
            pltpu.make_async_copy(w_ref.at[c], g_ref.at[c], wsem.at[c]).wait()

        def convert(t, _):
            c, r = t // (width // 16), t % (width // 16)
            at = pl.ds(pl.multiple_of(r * 16, 16), 16)
            high, low = split(g_ref[c, at, 0:end])
            whi[c, at, :] = high
            wlo[c, at, :] = low
            g_ref[c, at, :] = jnp.zeros((16, g_ref.shape[2]), f32)
            return 0

        lax.fori_loop(0, 2 * (width // 16), convert, 0)

    def weight(c, lo, hi):
        return whi[c, :, lo:hi], wlo[c, :, lo:hi]

    def vec(r):
        return vec_ref[r:r + 1, :]

    def normalize(v):
        center = v - jnp.mean(v, axis=-1, keepdims=True)
        inverse = lax.rsqrt(jnp.mean(center * center, axis=-1, keepdims=True) + norm_eps)
        return center * inverse, inverse

    def norm_back(grad, normed, inverse, gain):
        scaled = grad * gain
        return inverse * (scaled - jnp.mean(scaled, axis=-1, keepdims=True)
                          - normed * jnp.mean(scaled * normed, axis=-1, keepdims=True))

    def total(v):
        return jnp.sum(v, axis=0, keepdims=True)

    pad[0, 0:length, :] = x_ref[0]
    pad[1, 0:length, :] = cot_ref[0]
    x, cot = pad[0], pad[1]
    cot_hi[...], cot_lo[...] = split(cot)
    first, first_inverse = normalize(x)
    fo_hi[...], fo_lo[...] = split(first * vec(0) + vec(1))

    lane = lax.broadcasted_iota(jnp.int32, (rows, LANES), 1)
    sides = (lane < head, lane >= head)
    column = lax.broadcasted_iota(jnp.int32, (rows, rows), 1)
    score_scale = head ** (-0.5)

    def side(v, s):
        return jnp.where(sides[s], v, 0.0)

    def swap(v):
        return pltpu.roll(v, head, 1)

    def windows(c):
        w = [mixed[c, :, t * LANES:(t + 1) * LANES] for t in range(5)]
        third = side(w[3], 0) * score_scale, side(swap(w[3]), 0), side(w[4], 0)
        return [
            (side(w[0], 0) * score_scale, side(w[1], 0), side(w[2], 0)),
            (side(w[0], 1) * score_scale, side(w[1], 1), side(w[2], 1)),
            third,
        ]

    part[...] = jnp.zeros_like(part)

    def attend(c, _):
        mixed[c] = product((fo_hi[...], fo_lo[...]), weight(c, 0, qkv), 1, 0) + mb_ref[c]
        outs = []
        for h, (q, k, v) in enumerate(windows(c)):
            scores = product(split(q), split(k), 1, 1)
            scores = jnp.where(column < length, scores, MASKED)
            expon = jnp.exp(scores - jnp.max(scores, axis=-1, keepdims=True))
            probs = split(expon / jnp.sum(expon, axis=-1, keepdims=True))
            probs_hi[c, h], probs_lo[c, h] = probs
            outs.append(product_apart(probs, split(v), 1, 0))
        joined[c] = jnp.concatenate([swap(outs[2]), outs[0] + outs[1]], axis=1)
        part[...] += product(split(joined[c]), weight(c, 4 * LANES, attn), 1, 1)
        return 0

    lax.fori_loop(0, 2, attend, 0)
    middle = x + part[...] + vec(2)
    second, second_inverse = normalize(middle)
    so_hi[...], so_lo[...] = split(second * vec(3) + vec(4))

    part[...] = middle + vec(5)
    part2[...] = jnp.zeros_like(part2)

    def feed(c, _):
        so = (so_hi[...], so_lo[...])
        co = (cot_hi[...], cot_lo[...])
        hidden = product(so, weight(c, up, down), 1, 0) + eb_ref[c]
        share = 0.5 * (1.0 + lax.erf(hidden * (0.5 ** 0.5)))
        active = split(hidden * share)
        slope = share + hidden * jnp.exp(-0.5 * hidden * hidden) * 0.3989422804014327
        part[...] += product(active, weight(c, down, end), 1, 1)
        g_ref[c, :, down:end] += product(co, active, 0, 0)
        grad = product(co, weight(c, down, end), 1, 0) * slope
        sg_ref[c, 7:8, 0:hidden_local] += total(grad)
        grad = split(grad)
        g_ref[c, :, up:down] += product(so, grad, 0, 0)
        part2[...] += product(grad, weight(c, up, down), 1, 1)
        return 0

    lax.fori_loop(0, 2, feed, 0)
    y_ref[0] = part[0:length, :]

    grad_second = part2[...]
    sg_ref[0, 3:4, 0:width] += total(grad_second * second)
    sg_ref[0, 4:5, 0:width] += total(grad_second)
    sg_ref[0, 5:6, 0:width] += total(cot)
    grad_middle = cot + norm_back(grad_second, second, second_inverse, vec(3))
    sg_ref[0, 2:3, 0:width] += total(grad_middle)
    gm_hi[...], gm_lo[...] = split(grad_middle)
    part2[...] = grad_middle

    part[...] = jnp.zeros_like(part)

    def attend_back(c, _):
        gm = (gm_hi[...], gm_lo[...])
        fo = (fo_hi[...], fo_lo[...])
        grad_heads = product(gm, weight(c, 4 * LANES, attn), 1, 0)
        g_ref[c, :, 4 * LANES:attn] += product(gm, split(joined[c]), 0, 0)
        pair, single = grad_heads[:, LANES:], swap(grad_heads[:, :LANES])
        pair_out, single_out = joined[c, :, LANES:], swap(joined[c, :, :LANES])
        grad_outs = (side(pair, 0), side(pair, 1), side(single, 0))
        outs = (pair_out, pair_out, single_out)
        grads = []
        for h, (q, k, v) in enumerate(windows(c)):
            grad_out = grad_outs[h]
            row = jnp.sum(grad_out * outs[h], axis=-1, keepdims=True)
            grad_out = split(grad_out)
            grad_probs = product(grad_out, split(v), 1, 1)
            probs = (probs_hi[c, h], probs_lo[c, h])
            grad_v = product(probs, grad_out, 0, 0)
            grad_scores = split((probs[0].astype(f32) + probs[1].astype(f32)) * (grad_probs - row))
            grad_q = product_apart(grad_scores, split(k), 1, 0) * score_scale
            grad_k = product(grad_scores, split(q), 0, 0)
            grads.append((grad_q, grad_k, grad_v))
        one, two, three = grads
        grad_mixed = jnp.concatenate(
            [one[0] + two[0], one[1] + two[1], one[2] + two[2], three[0] + swap(three[1]), three[2]], axis=1)
        sg_ref[c, 6:7, 0:qkv] += total(grad_mixed)
        grad_mixed = split(grad_mixed)
        g_ref[c, :, 0:qkv] += product(fo, grad_mixed, 0, 0)
        part[...] += product(grad_mixed, weight(c, 0, qkv), 1, 1)
        return 0

    lax.fori_loop(0, 2, attend_back, 0)
    grad_first = part[...]
    sg_ref[0, 0:1, 0:width] += total(grad_first * first)
    sg_ref[0, 1:2, 0:width] += total(grad_first)
    gx_ref[0] = (part2[...] + norm_back(grad_first, first, first_inverse, vec(0)))[0:length, :]


def run_layer(base, inputs, cotangent, weights, vectors, mixed_bias, expand_bias, heads, head):
    images, length, width = inputs.shape
    own = images // 2
    rows = -(-length // 16) * 16
    columns = weights.shape[-1]
    hidden_local = expand_bias.shape[-1]
    end = 6 * LANES + 2 * hidden_local
    image = pl.BlockSpec((1, length, width), lambda i, b: (b[0] + i, 0, 0))

    def whole(shape):
        return pl.BlockSpec(shape, lambda i, b: (0,) * len(shape))

    act = pltpu.VMEM((rows, width), bf16)
    return pl.pallas_call(
        functools.partial(layer_kernel, length, heads, head),
        grid_spec=pltpu.PrefetchScalarGridSpec(
            num_scalar_prefetch=1,
            grid=(own,),
            in_specs=[image, image, pl.BlockSpec(memory_space=pl.ANY), whole(vectors.shape),
                      whole(mixed_bias.shape), whole(expand_bias.shape)],
            out_specs=[image, image, whole((2, width, columns)), whole((2, 8, hidden_local))],
            scratch_shapes=[
                pltpu.VMEM((2, width, end), bf16), pltpu.VMEM((2, width, end), bf16),
                pltpu.SemaphoreType.DMA((2,)),
                pltpu.VMEM((2, rows, width), f32),
                pltpu.VMEM((2, rows, 5 * LANES), f32),
                pltpu.VMEM((2, heads, rows, rows), bf16), pltpu.VMEM((2, heads, rows, rows), bf16),
                pltpu.VMEM((2, rows, 2 * LANES), f32),
                act, act, act, act, act, act, act, act,
                pltpu.VMEM((rows, width), f32), pltpu.VMEM((rows, width), f32),
            ],
        ),
        out_shape=[
            jax.ShapeDtypeStruct(inputs.shape, f32), jax.ShapeDtypeStruct(inputs.shape, f32),
            jax.ShapeDtypeStruct((2, width, columns), f32), jax.ShapeDtypeStruct((2, 8, hidden_local), f32),
        ],
        compiler_params=pltpu.CompilerParams(
            dimension_semantics=("arbitrary",), vmem_limit_bytes=60 * 2**20),
        name="layer",
    )(base, inputs, cotangent, weights, vectors, mixed_bias, expand_bias)


def rings(n):
    side = max(k for k in range(1, n + 1) if n % (k * k) == 0 and n // (k * k) >= k)
    return n // (side * side), side, side


def place(sizes):
    first, side, _ = sizes
    core, me = lax.axis_index("mp"), lax.axis_index("dp")
    a, b, c = me // (side * side), (me // side) % side, me % side

    def at(slab, sign=1, of=core):
        i, j, k = slab
        i, j, k = (sign * i) % first, (sign * j) % side, (sign * k) % side
        ahead_b = j * of + k * (1 - of)
        ahead_c = k * of + j * (1 - of)
        return (((a + i) % first) * side + (b + ahead_b) % side) * side + (c + ahead_c) % side

    return core, at


UNITS = ((1, 0, 0), (0, 1, 0), (0, 0, 1))


def plus(slab, unit):
    return tuple(s + u for s, u in zip(slab, unit))


def sends(slab, sizes):
    return [r for r in range(3) if not any(slab[r + 1:]) and slab[r] + 1 < sizes[r]]


def arrival_order(sizes):
    cost, free, heap, order = (2.0, 1.5, 1.5), [0.0] * 3, [(0.0, (0, 0, 0))], []
    while heap:
        now, slab = heapq.heappop(heap)
        order.append(slab)
        for r in sends(slab, sizes):
            free[r] = max(now, free[r]) + cost[r]
            heapq.heappush(heap, (free[r], plus(slab, UNITS[r])))
    return order


def slab_id(slab, sizes):
    return (slab[0] * sizes[1] + slab[1]) * sizes[2] + slab[2]


def greet(core, at, sign):
    barrier = pltpu.get_barrier_semaphore()
    for unit in UNITS:
        pl.semaphore_signal(barrier, inc=1, device_id={"dp": at(unit, sign)})
    pl.semaphore_signal(barrier, inc=1, device_id={"mp": 1 - core})
    pl.semaphore_wait(barrier, 4)


def gather_kernel(sizes, slab_ref, out_ref, send_sem, recv_sem, swap_send, swap_recv, own_sem):
    core, at = place(sizes)
    number = functools.partial(slab_id, sizes=sizes)
    greet(core, at, -1)

    def landing(slab, of):
        return out_ref.at[of, at(slab, -1, of)]

    started = []
    own = pltpu.make_async_copy(slab_ref, landing((0, 0, 0), core), own_sem)
    for slab in arrival_order(sizes):
        spot = landing(slab, core)
        if any(slab):
            pltpu.make_async_remote_copy(
                src_ref=spot, dst_ref=spot, send_sem=send_sem.at[0, 0], recv_sem=recv_sem.at[number(slab)],
                device_id={"mp": 1 - core}).wait_recv()
        source = spot if any(slab) else slab_ref
        for r in reversed(sends(slab, sizes)):
            copy = pltpu.make_async_remote_copy(
                src_ref=source, dst_ref=spot, send_sem=send_sem.at[r, number(slab)],
                recv_sem=recv_sem.at[number(plus(slab, UNITS[r]))], device_id={"dp": at(UNITS[r])})
            copy.start()
            started.append(copy)
        copy = pltpu.make_async_remote_copy(
            src_ref=source, dst_ref=spot, send_sem=swap_send.at[number(slab)], recv_sem=swap_recv.at[number(slab)],
            device_id={"mp": 1 - core})
        copy.start()
        started.append(copy)
        if not any(slab):
            own.start()
    for slab in arrival_order(sizes):
        spot = landing(slab, 1 - core)
        pltpu.make_async_remote_copy(
            src_ref=spot, dst_ref=spot, send_sem=swap_send.at[0], recv_sem=swap_recv.at[number(slab)],
            device_id={"mp": 1 - core}).wait_recv()
    for copy in started:
        copy.wait_send()
    own.wait()


def gather(slab, n):
    sizes = rings(n)
    return pl.pallas_call(
        functools.partial(gather_kernel, sizes),
        out_shape=jax.ShapeDtypeStruct((2, n) + slab.shape, f32),
        in_specs=[pl.BlockSpec(memory_space=pltpu.VMEM)],
        out_specs=pl.BlockSpec(memory_space=pl.ANY),
        scratch_shapes=[
            pltpu.SemaphoreType.DMA((3, n)), pltpu.SemaphoreType.DMA((n,)),
            pltpu.SemaphoreType.DMA((n,)), pltpu.SemaphoreType.DMA((n,)), pltpu.SemaphoreType.DMA,
        ],
        compiler_params=pltpu.CompilerParams(collective_id=0, has_side_effects=True),
        name="gather",
    )(slab)


def scatter_kernel(sizes, g_ref, y_in, gx_in, out_ref, y_ref, gx_ref,
                   acc, swapped, landed, load_sem, send_sem, recv_sem, swap_send, swap_recv, image_send, image_recv):
    del y_in, gx_in
    core, at = place(sizes)
    number = functools.partial(slab_id, sizes=sizes)
    greet(core, at, -1)
    first, side, _ = sizes
    order = [(i, j, k) for k in reversed(range(side)) for j in reversed(range(side)) for i in reversed(range(first))]
    own = y_ref.shape[0] // 2
    started, loads, images = [], {}, []
    for slab in order:
        s = number(slab)
        copy = pltpu.make_async_remote_copy(
            src_ref=g_ref.at[1 - core, at(slab, 1, 1 - core)], dst_ref=swapped.at[s],
            send_sem=swap_send.at[s], recv_sem=swap_recv.at[s], device_id={"mp": 1 - core})
        copy.start()
        started.append(copy)
        loads[slab] = pltpu.make_async_copy(g_ref.at[core, at(slab)], acc.at[s], load_sem.at[s])
        loads[slab].start()
    for t, ref in enumerate((y_ref, gx_ref)):
        mine = ref.at[pl.ds(core * own, own)]
        copy = pltpu.make_async_remote_copy(
            src_ref=mine, dst_ref=mine, send_sem=image_send.at[t], recv_sem=image_recv.at[t],
            device_id={"mp": 1 - core})
        copy.start()
        started.append(copy)
        theirs = ref.at[pl.ds((1 - core) * own, own)]
        images.append(pltpu.make_async_remote_copy(
            src_ref=theirs, dst_ref=theirs, send_sem=image_send.at[t], recv_sem=image_recv.at[t],
            device_id={"mp": 1 - core}))

    def arrived(buffer, spot, sem):
        pltpu.make_async_remote_copy(
            src_ref=buffer.at[spot], dst_ref=buffer.at[spot], send_sem=swap_send.at[0], recv_sem=sem,
            device_id={"mp": 1 - core}).wait_recv()
        return buffer[spot]

    for slab in order:
        s = number(slab)
        loads[slab].wait()
        value = acc[s] + arrived(swapped, s, swap_recv.at[s])
        for r in range(3):
            if not any(slab[r + 1:]) and slab[r] + 1 < sizes[r]:
                spot = number(plus(slab, UNITS[r]))
                value = value + arrived(landed, spot - 1, recv_sem.at[spot])
        if any(slab):
            acc[s] = value
            r = max(q for q in range(3) if slab[q])
            copy = pltpu.make_async_remote_copy(
                src_ref=acc.at[s], dst_ref=landed.at[s - 1], send_sem=send_sem.at[s], recv_sem=recv_sem.at[s],
                device_id={"dp": at(UNITS[r])})
            copy.start()
            started.append(copy)
        else:
            out_ref[...] = value
    for copy in images:
        copy.wait_recv()
    for copy in started:
        copy.wait_send()


def scatter(grads, block_out, input_gradient, n):
    sizes = rings(n)
    slab = grads.shape[2:]
    anywhere = pl.BlockSpec(memory_space=pl.ANY)
    return pl.pallas_call(
        functools.partial(scatter_kernel, sizes),
        out_shape=[jax.ShapeDtypeStruct(slab, f32), jax.ShapeDtypeStruct(block_out.shape, f32),
                   jax.ShapeDtypeStruct(input_gradient.shape, f32)],
        in_specs=[anywhere] * 3,
        out_specs=[pl.BlockSpec(memory_space=pltpu.VMEM), anywhere, anywhere],
        input_output_aliases={1: 1, 2: 2},
        scratch_shapes=[
            pltpu.VMEM((n,) + slab, f32), pltpu.VMEM((n,) + slab, f32), pltpu.VMEM((n - 1,) + slab, f32),
            pltpu.SemaphoreType.DMA((n,)), pltpu.SemaphoreType.DMA((n,)), pltpu.SemaphoreType.DMA((n,)),
            pltpu.SemaphoreType.DMA((n,)), pltpu.SemaphoreType.DMA((n,)),
            pltpu.SemaphoreType.DMA((2,)), pltpu.SemaphoreType.DMA((2,)),
        ],
        compiler_params=pltpu.CompilerParams(
            collective_id=1, has_side_effects=True, vmem_limit_bytes=60 * 2**20),
        name="scatter",
    )(grads, block_out, input_gradient)


def pack_attention(mixer, output):
    head = mixer.shape[2] // 3
    pair = 2 * head
    out = output.T
    q, k, v = mixer[:, 0], mixer[:, 1], mixer[:, 2]
    return jnp.concatenate([q[:, :pair], k[:, :pair], v[:, :pair], q[:, pair:], k[:, pair:], v[:, pair:],
                            out[:, pair:], out[:, :pair]], axis=1)


def unpack_attention(block, head):
    pair = 2 * head
    cut = [block[:, t * head:(t + 1) * head] for t in range(12)]
    mixer = jnp.stack([jnp.concatenate(t, axis=1) for t in (
        (cut[0], cut[1], cut[6]), (cut[2], cut[3], cut[7]), (cut[4], cut[5], cut[8]))], axis=1)
    output = jnp.concatenate([cut[10], cut[11], cut[9]], axis=1).T
    return mixer, output


SMALL = ("first_gain", "first_shift", "output_bias", "second_gain", "second_shift", "reduce_bias",
         "mixer_bias", "expand_bias")


def pack_small(values):
    return jnp.concatenate([values[name].reshape(-1) for name in SMALL])


def unpack_small(flat, like):
    out, start = {}, 0
    for name in SMALL:
        size = like[name].size
        out[name] = flat[start:start + size].reshape(like[name].shape)
        start += size
    return out


def adam_update(param, grad, momentum, variance, decay):
    momentum_next = beta_one * momentum + (1.0 - beta_one) * grad
    variance_next = beta_two * variance + (1.0 - beta_two) * grad * grad
    mean_hat = momentum_next / (1.0 - beta_one**step_count)
    square_hat = variance_next / (1.0 - beta_two**step_count)
    stepped = param - learn_rate * (mean_hat / (jnp.sqrt(square_hat) + adam_eps) + decay * param)
    return (stepped, momentum_next, variance_next)


NAMES = ("first_gain", "first_shift", "mixer_weight", "mixer_bias", "output_weight", "output_bias", "second_gain",
         "second_shift", "expand_weight", "expand_bias", "reduce_weight", "reduce_bias")
DECAYED = ("mixer_weight", "output_weight", "expand_weight", "reduce_weight")


def per_device(inputs, cotangent, *rest):
    n = lax.axis_size("dp")
    scale = (n * inputs.shape[0] * inputs.shape[1]) ** (-0.5)
    params = dict(zip(NAMES, rest[:12]))
    momenta = dict(zip(NAMES, rest[12:24]))
    variances = dict(zip(NAMES, rest[24:]))
    share, width = params["first_gain"].shape[0], inputs.shape[2]
    heads, piece = params["mixer_bias"].shape[1:]
    head = piece * n
    hidden_local = params["expand_weight"].shape[1]
    end = 6 * LANES + 2 * hidden_local

    small = pack_small(params)
    count = small.shape[0]
    slab = jnp.concatenate([
        pack_attention(params["mixer_weight"], params["output_weight"]),
        params["expand_weight"], params["reduce_weight"].T,
        jnp.pad(small, (0, share * LANES - count)).reshape(share, LANES)], axis=1)
    columns = slab.shape[1]
    gathered = gather(slab, n)

    flat = gathered[:, :, :, end:].reshape(2, n, share * LANES)[:, :, :count]
    vectors = jnp.pad(flat[0, :, :6 * share].reshape(n, 6, share).transpose(1, 0, 2).reshape(6, width),
                      ((0, 2), (0, 0)))
    bias = flat[:, :, 6 * share:7 * share].reshape(2, n, 2, heads, piece).transpose(0, 2, 3, 1, 4)
    bias = bias.reshape(2, 2, heads * head)
    q, v, none = bias[:, 0], bias[:, 1], jnp.zeros((2, 2 * head), f32)
    mixed_bias = jnp.concatenate([q[:, :2 * head], none, v[:, :2 * head], q[:, 2 * head:], none[:, :head],
                                  v[:, 2 * head:], none[:, :head]], axis=1)[:, None]
    expand_bias = flat[:, :, 7 * share:].reshape(2, n, -1, piece).transpose(0, 2, 1, 3).reshape(2, 1, -1)

    base = (lax.axis_index("mp") * (inputs.shape[0] // 2)).astype(jnp.int32).reshape(1)
    block_out, input_gradient, grads, small_grads = run_layer(
        base, inputs, cotangent, gathered.reshape(2, width, columns), vectors, mixed_bias, expand_bias, heads, head)

    six = jnp.broadcast_to(small_grads[0, :6, :width].reshape(1, 6, n, share), (2, 6, n, share))
    six = six * (jnp.arange(2) == 0).astype(f32).reshape(2, 1, 1, 1)
    total = small_grads[:1, :6, :width].reshape(6, n, share).transpose(1, 0, 2).reshape(n, 6 * share)
    row = small_grads[:, 6, :5 * LANES]
    bias = jnp.stack([
        jnp.concatenate([row[:, :2 * head], row[:, 6 * head:7 * head]], axis=1),
        jnp.concatenate([row[:, 4 * head:6 * head], row[:, 8 * head:9 * head]], axis=1)], axis=1)
    bias = bias.reshape(2, 2, heads, n, piece).transpose(0, 3, 1, 2, 4).reshape(2, n, share)
    hidden = small_grads[:, 7].reshape(2, hidden_local // head, n, piece).transpose(0, 2, 1, 3).reshape(2, n, -1)
    packed = jnp.concatenate([jnp.broadcast_to(total[None], (2,) + total.shape), bias, hidden], axis=2)
    packed = jnp.pad(packed, ((0, 0), (0, 0), (0, share * LANES - count))).reshape(2, n, share, LANES)
    grads = lax.dynamic_update_slice(grads.reshape(2, n, share, columns), packed, (0, 0, 0, end))

    summed, block_out, input_gradient = scatter(grads, block_out, input_gradient, n)
    summed = summed * scale
    mixer, output = unpack_attention(summed[:, :6 * LANES], head)
    gradients = unpack_small(summed[:, end:].reshape(-1), params)
    gradients.update(mixer_weight=mixer, output_weight=output,
                     expand_weight=summed[:, 6 * LANES:6 * LANES + hidden_local],
                     reduce_weight=summed[:, 6 * LANES + hidden_local:end].T)
    results = [adam_update(params[m], gradients[m], momenta[m], variances[m], weight_decay if m in DECAYED else 0.0)
               for m in NAMES]
    return (block_out, input_gradient, *(gradients[m] for m in NAMES), *(r[0] for r in results),
            *(r[1] for r in results), *(r[2] for r in results))


def solution(mesh):
    images = P("dp", None, None)
    entries = (P("dp"), P("dp"), P("dp", None, "mp"), P(None, "mp", "dp"), P("mp", "dp"), P("dp"), P("dp"), P("dp"),
               P("dp", "mp"), P("mp", "dp"), P("mp", "dp"), P("dp"))
    return jax.shard_map(per_device, mesh=mesh, in_specs=(images, images) + entries * 3,
                         out_specs=(images, images) + entries * 4, check_vma=False)
```

time: 1020 us -> 201 us (0.20)
  waiting for transfers between devices: 438 us -> 0 us
  blocking collectives: 312 us -> 0 us
  matrix products: 174 us -> 0 us
  Pallas kernels: 0 us -> 165 us
  other arithmetic: 46.6 us -> 4.89 us
  between operations: 18.6 us -> 1.48 us
    reduce_scatter x4 -> x0, waiting for transfers between devices: 393 us -> none  [the longest x1 128 us: per_device(): lax.psum_scatter(grad_mixer, 'dp', scatter_dimension=0, tiled=True)]
    dot_general x18 -> x0, matrix products: 174 us -> none  [the longest x1 20 us: per_device(): jnp.einsum('bscf,dcf->bsd', grad_mixed, back_mixer, precision=highest)]
    all_gather x4 -> x0, blocking collectives: 165 us -> none  [the longest x1 48.5 us: per_device(): lax.all_gather(mixer_weight, 'dp', axis=0, tiled=True)]
    pallas_call x0 -> x3, Pallas kernels: none -> 165 us  [the longest x1 76.5 us: run_layer(): pl.pallas_call(functools.partial(layer_kernel, length, heads, head), grid...]
    unnamed x2 -> x0, blocking collectives: 147 us -> none
    all_gather x2 -> x0, waiting for transfers between devices: 44.5 us -> none  [the longest x1 31.6 us: per_device(): lax.all_gather(reduce_weight, 'dp', axis=1, tiled=True)]
    reduce_sum x10 -> x0, other arithmetic: 18.5 us -> none  [the longest x2 6.54 us: norm_backward(): grad_gain = jnp.sum(grad_out * normed, axis=(0, 1))]
    another operation x1 -> x4, other arithmetic: 11.8 us -> 0.03 us  [the longest x3 0.02 us: unpack_attention(): jnp.stack([jnp.concatenate(t, axis=1) for t in ((cut[0], cut[1], cut[6]),...]
  transfers between devices with their start and end apart: 9 -> 0, of which waited for: 6 -> 0; matrix products, arithmetic and copies ran while one was open for 15% -> 0% of each run, Pallas kernels for 0% -> 0%
where the time goes in v1:
time: 201 us
  Pallas kernels  165 us (82%)
  local copies, waits for them, and re-layouts  29.6 us (15%)
  other arithmetic  4.89 us (2%)
    pallas_call x1, Pallas kernels, run_layer(): pl.pallas_call(functools.partial(layer_kernel, length, heads, head), grid...  76.5 us
    pallas_call x1, Pallas kernels, scatter(): pl.pallas_call(functools.partial(scatter_kernel, sizes), out_shape=[jax.S...  44.7 us
    pallas_call x1, Pallas kernels, gather(): pl.pallas_call(functools.partial(gather_kernel, sizes), out_shape=jax.Sha...  43.6 us
    unnamed x95, local copies, waits for them, and re-layouts  15.6 us
    sub x8, other arithmetic, adam_update(): param - learn_rate * (mean_hat / (jnp.sqrt(square_hat) + adam_eps) + deca...  4.73 us

profile of v1, /device:TPU:0, one launch (start us, length us, event | category | flops | bytes accessed | tf_op | source)
XLA Modules:
  0.0 200.8 jit_solution(17080698941488488735)
XLA Ops:
  0.7 0.7 copy.171
  1.4 0.1 reshape.164
  1.5 0.8 copy.172
  2.3 0.1 reshape.165
  2.3 0.8 concatenate.35
  3.2 0.7 slice.228
  3.9 0.7 slice.227
  4.6 0.8 slice_bitcast_fusion.1
  5.4 1.7 concatenate.36.slab_ref
  7.1 3.8 %copy.180.x_ref = f32[8,197,384]{2,1,0:T(8,128)} copy(f32[8,197,384]{2,0,1:T(8,128)} %param.38) | data formatting | bytes 4841472 | tf_op args[0]
  10.9 1.9 copy.181.cot_ref
  12.8 43.6 %gather.1 = f32[2,16,24,2432]{3,2,1,0:T(8,128)} custom-call(f32[24,2432]{1,0:T(8,128)} %concatenate.36.slab_ref), custom_call_target="tpu_custom_call" | custom-call | tf_op jit(solution)/shard_map/gather/pallas_call | solution.py:350
  56.5 1.0 slice.183
  57.5 0.1 reshape.168
  57.6 0.1 slice.230
  57.6 0.1 copy.203
  57.7 0.1 slice.237
  57.8 0.1 copy.204
  57.9 0.1 reshape_squeeze.6
  58.0 0.1 reshape.169
  58.1 0.6 pad.13.vec_ref
  58.7 0.1 copy.200
  58.8 0.1 reshape.180
  59.0 0.1 concatenate.37
  59.1 0.6 broadcast_in_dim.14.mb_ref
  59.7 0.2 copy.179
  59.9 0.7 reshape.181.eb_ref
  60.6 76.5 %layer.1 = (f32[8,197,384]{2,1,0:T(8,128)}, f32[8,197,384]{2,1,0:T(8,128)}, f32[2,384,2432]{2,1,0:T(8,128)}, f32[2,8,768]{2,1,0:T(8,128)}) custom-call(s32[1]{0:T(128)} %bitcast.base, f32[8,197,384]{2,1,0:T(8,128)} %copy.180.x_ref, f32[8,197,384]{2,1,0:T(8,128)} %copy.181.cot_ref, f32[2,384,2432]{2,1,0:T(8,128)} %bitcast.61, f32[8,384]{1,0:T(8,128)} %pad.13.vec_ref, ...), custom_call_target="tpu_custom_call" | custom-call | tf_op jit(solution)/shard_map/layer/pallas_call | solution.py:225
  137.2 0.8 slice.194
  138.0 0.8 slice_reduce_fusion
  138.8 0.7 slice.193
  139.5 0.1 reshape.175
  139.7 0.1 broadcast_in_dim.15
  139.7 0.1 stack.21
  139.8 0.1 copy.184
  139.9 0.1 stack.22
  140.1 0.1 copy.185
  140.2 0.1 copy.187
  140.3 0.2 reshape_squeeze.7
  140.5 0.2 copy.186
  140.7 0.1 copy.188
  140.7 0.1 select_maximum_fusion
  140.8 0.1 copy.206
  140.9 0.8 bitcast_dynamic-update-slice_fusion.g_ref
  141.8 44.7 %scatter.1 = (f32[24,2432]{1,0:T(8,128)}, f32[8,197,384]{2,1,0:T(8,128)}, f32[8,197,384]{2,1,0:T(8,128)}) custom-call(f32[2,16,24,2432]{3,2,1,0:T(8,128)} %bitcast_dynamic-update-slice_fusion.g_ref, f32[8,197,384]{2,1,0:T(8,128)} %get-tuple-element.59.y_in, f32[8,197,384]{2,1,0:T(8,128)} %get-tuple-element.60.gx_in), custom_call_target="tpu_custom_call", output_to_operand_aliasing={{1}: (1, {}), {2}: (2, {})} | custom-call | tf_op jit(solution)/shard_map/scatter/pallas_call | solution.py:429
  186.5 0.0 copy-start.22
  186.5 0.0 copy-start.28
  186.9 3.7 %copy.194 = f32[8,197,384]{2,0,1:T(8,128)} copy(f32[8,197,384]{2,1,0:T(8,128)} %get-tuple-element.214) | data formatting | bytes 4841472
  190.7 0.1 fusion.27
  190.8 0.6 multiply_subtract_fusion.10
  191.5 0.7 multiply_subtract_fusion.6
  192.3 0.6 multiply_subtract_fusion.3
  192.9 0.7 multiply_subtract_fusion.2
  193.7 0.7 multiply_subtract_fusion
  194.4 0.7 multiply_subtract_fusion.1
  195.1 0.4 slice.217
  195.5 0.1 copy.205
  195.6 0.6 multiply_subtract_fusion.5
  196.3 0.3 slice.209
  196.6 0.6 copy.197
  197.2 0.6 copy.198
  197.8 0.6 copy.199
  198.4 0.6 copy.196
  198.9 1.9 copy.195
  (108 shorter events, 0.4 us)
Async XLA Ops:
  7.1 3.8 %copy-start.1 = (f32[8,197,384]{2,0,1:T(8,128)S(1)}, f32[8,197,384]{2,0,1:T(8,128)}, u32[]{:S(2)}) copy-start(f32[8,197,384]{2,0,1:T(8,128)} %param.39) | copy-start | bytes 7262212
  186.5 4.1 %copy-start.5 = (f32[24,2432]{1,0:T(8,128)S(1)}, f32[24,2432]{1,0:T(8,128)}, u32[]{:S(2)}) copy-start(f32[24,2432]{1,0:T(8,128)} %get-tuple-element.63) | copy-start | bytes 700420
  186.5 4.3 %copy-start.22 = (f32[24]{0:T(128)S(1)}, f32[24]{0:T(128)}, u32[]{:S(2)}) copy-start(f32[24]{0:T(128)} %param.40) | copy-start | bytes 292
  186.5 4.3 %copy-start.23 = (f32[24]{0:T(128)S(1)}, f32[24]{0:T(128)}, u32[]{:S(2)}) copy-start(f32[24]{0:T(128)} %param.41) | copy-start | bytes 292
  186.5 4.2 %copy-start.28 = (f32[24]{0:T(128)S(1)}, f32[24]{0:T(128)}, u32[]{:S(2)}) copy-start(f32[24]{0:T(128)} %param.53) | copy-start | bytes 292
  186.5 4.2 %copy-start.29 = (f32[24]{0:T(128)S(1)}, f32[24]{0:T(128)}, u32[]{:S(2)}) copy-start(f32[24]{0:T(128)} %param.65) | copy-start | bytes 292
  186.6 4.2 %copy-start.30 = (f32[24]{0:T(128)S(1)}, f32[24]{0:T(128)}, u32[]{:S(2)}) copy-start(f32[24]{0:T(128)} %param.64) | copy-start | bytes 292
  186.6 4.2 %copy-start.31 = (f32[24]{0:T(128)S(1)}, f32[24]{0:T(128)}, u32[]{:S(2)}) copy-start(f32[24]{0:T(128)} %param.52) | copy-start | bytes 292
  186.6 4.9 %copy-start.24 = (f32[24]{0:T(128)S(1)}, f32[24]{0:T(128)}, u32[]{:S(2)}) copy-start(f32[24]{0:T(128)} %param.45) | copy-start | bytes 292
  186.6 4.8 %copy-start.25 = (f32[24]{0:T(128)S(1)}, f32[24]{0:T(128)}, u32[]{:S(2)}) copy-start(f32[24]{0:T(128)} %param.46) | copy-start | bytes 292
  186.6 4.8 %copy-start.26 = (f32[24]{0:T(128)S(1)}, f32[24]{0:T(128)}, u32[]{:S(2)}) copy-start(f32[24]{0:T(128)} %param.47) | copy-start | bytes 292
  186.6 4.8 %copy-start.27 = (f32[24]{0:T(128)S(1)}, f32[24]{0:T(128)}, u32[]{:S(2)}) copy-start(f32[24]{0:T(128)} %param.51) | copy-start | bytes 292
  186.6 4.8 %copy-start.32 = (f32[24]{0:T(128)S(1)}, f32[24]{0:T(128)}, u32[]{:S(2)}) copy-start(f32[24]{0:T(128)} %param.63) | copy-start | bytes 292
  186.6 4.8 %copy-start.33 = (f32[24]{0:T(128)S(1)}, f32[24]{0:T(128)}, u32[]{:S(2)}) copy-start(f32[24]{0:T(128)} %param.75) | copy-start | bytes 292
  186.6 4.8 %copy-start.34 = (f32[24]{0:T(128)S(1)}, f32[24]{0:T(128)}, u32[]{:S(2)}) copy-start(f32[24]{0:T(128)} %param.71) | copy-start | bytes 292
  186.7 4.8 %copy-start.35 = (f32[24]{0:T(128)S(1)}, f32[24]{0:T(128)}, u32[]{:S(2)}) copy-start(f32[24]{0:T(128)} %param.59) | copy-start | bytes 292
  186.7 4.8 %copy-start.36 = (f32[24]{0:T(128)S(1)}, f32[24]{0:T(128)}, u32[]{:S(2)}) copy-start(f32[24]{0:T(128)} %param.70) | copy-start | bytes 292
  186.7 4.8 %copy-start.37 = (f32[24]{0:T(128)S(1)}, f32[24]{0:T(128)}, u32[]{:S(2)}) copy-start(f32[24]{0:T(128)} %param.58) | copy-start | bytes 292
  186.7 4.8 %copy-start.38 = (f32[24]{0:T(128)S(1)}, f32[24]{0:T(128)}, u32[]{:S(2)}) copy-start(f32[24]{0:T(128)} %param.69) | copy-start | bytes 292
  186.7 4.8 %copy-start.39 = (f32[24]{0:T(128)S(1)}, f32[24]{0:T(128)}, u32[]{:S(2)}) copy-start(f32[24]{0:T(128)} %param.57) | copy-start | bytes 292
  186.7 5.5 %copy-start.6 = (f32[192,24]{0,1:T(8,128)S(1)}, f32[192,24]{0,1:T(8,128)}, u32[]{:S(2)}) copy-start(f32[192,24]{0,1:T(8,128)} %param.44) | copy-start | bytes 55300
  186.7 5.5 %copy-start.13 = (f32[192,24]{0,1:T(8,128)S(1)}, f32[192,24]{0,1:T(8,128)}, u32[]{:S(2)}) copy-start(f32[192,24]{0,1:T(8,128)} %param.56) | copy-start | bytes 55300
  186.7 5.5 %copy-start.14 = (f32[192,24]{0,1:T(8,128)S(1)}, f32[192,24]{0,1:T(8,128)}, u32[]{:S(2)}) copy-start(f32[192,24]{0,1:T(8,128)} %param.68) | copy-start | bytes 55300
  186.8 6.2 %copy-start.2 = (f32[24,3,192]{2,0,1:T(8,128)S(1)}, f32[24,3,192]{2,0,1:T(8,128)}, u32[]{:S(2)}) copy-start(f32[24,3,192]{2,0,1:T(8,128)} %param.42) | copy-start | bytes 165892
  186.8 6.2 %copy-start.7 = (f32[24,3,192]{2,0,1:T(8,128)S(1)}, f32[24,3,192]{2,0,1:T(8,128)}, u32[]{:S(2)}) copy-start(f32[24,3,192]{2,0,1:T(8,128)} %param.54) | copy-start | bytes 165892
  186.8 6.1 %copy-start.8 = (f32[24,3,192]{2,0,1:T(8,128)S(1)}, f32[24,3,192]{2,0,1:T(8,128)}, u32[]{:S(2)}) copy-start(f32[24,3,192]{2,0,1:T(8,128)} %param.66) | copy-start | bytes 165892
  186.8 6.9 %copy-start.3 = (f32[768,24]{0,1:T(8,128)S(1)}, f32[768,24]{0,1:T(8,128)}, u32[]{:S(2)}) copy-start(f32[768,24]{0,1:T(8,128)} %param.50) | copy-start | bytes 221188
  186.8 6.9 %copy-start.9 = (f32[768,24]{0,1:T(8,128)S(1)}, f32[768,24]{0,1:T(8,128)}, u32[]{:S(2)}) copy-start(f32[768,24]{0,1:T(8,128)} %param.62) | copy-start | bytes 221188
  186.8 6.8 %copy-start.10 = (f32[768,24]{0,1:T(8,128)S(1)}, f32[768,24]{0,1:T(8,128)}, u32[]{:S(2)}) copy-start(f32[768,24]{0,1:T(8,128)} %param.74) | copy-start | bytes 221188
  186.8 7.6 %copy-start.4 = (f32[24,768]{1,0:T(8,128)S(1)}, f32[24,768]{1,0:T(8,128)}, u32[]{:S(2)}) copy-start(f32[24,768]{1,0:T(8,128)} %param.48) | copy-start | bytes 221188
  186.8 7.6 %copy-start.11 = (f32[24,768]{1,0:T(8,128)S(1)}, f32[24,768]{1,0:T(8,128)}, u32[]{:S(2)}) copy-start(f32[24,768]{1,0:T(8,128)} %param.60) | copy-start | bytes 221188
  186.9 7.5 %copy-start.12 = (f32[24,768]{1,0:T(8,128)S(1)}, f32[24,768]{1,0:T(8,128)}, u32[]{:S(2)}) copy-start(f32[24,768]{1,0:T(8,128)} %param.72) | copy-start | bytes 221188
  190.6 5.0 %copy-start.16 = (f32[12,4]{0,1:T(4,128)S(1)}, f32[12,4]{0,1:T(4,128)}, u32[]{:S(2)}) copy-start(f32[12,4]{0,1:T(4,128)} %param.49) | copy-start | bytes 580
  190.6 5.0 %copy-start.20 = (f32[12,4]{0,1:T(4,128)S(1)}, f32[12,4]{0,1:T(4,128)}, u32[]{:S(2)}) copy-start(f32[12,4]{0,1:T(4,128)} %param.61) | copy-start | bytes 580
  190.6 5.0 %copy-start.21 = (f32[12,4]{0,1:T(4,128)S(1)}, f32[12,4]{0,1:T(4,128)}, u32[]{:S(2)}) copy-start(f32[12,4]{0,1:T(4,128)} %param.73) | copy-start | bytes 580
  190.6 6.0 %copy-start.15 = (f32[2,3,4]{2,0,1:T(2,128)S(1)}, f32[2,3,4]{2,0,1:T(2,128)}, u32[]{:S(2)}) copy-start(f32[2,3,4]{2,0,1:T(2,128)} %param.43) | copy-start | bytes 292
  190.6 6.0 %copy-start.18 = (f32[2,3,4]{2,0,1:T(2,128)S(1)}, f32[2,3,4]{2,0,1:T(2,128)}, u32[]{:S(2)}) copy-start(f32[2,3,4]{2,0,1:T(2,128)} %param.55) | copy-start | bytes 292
  190.6 6.0 %copy-start.19 = (f32[2,3,4]{2,0,1:T(2,128)S(1)}, f32[2,3,4]{2,0,1:T(2,128)}, u32[]{:S(2)}) copy-start(f32[2,3,4]{2,0,1:T(2,128)} %param.67) | copy-start | bytes 292
  190.6 8.3 %copy-start = (f32[8,197,384]{2,1,0:T(8,128)S(1)}, f32[8,197,384]{2,1,0:T(8,128)}, u32[]{:S(2)}) copy-start(f32[8,197,384]{2,1,0:T(8,128)} %get-tuple-element.215) | copy-start | bytes 7262212
  195.6 5.2 %copy-start.17 = (f32[12,4]{0,1:T(4,128)}, f32[12,4]{0,1:T(4,128)S(1)}, u32[]{:S(2)}) copy-start(f32[12,4]{0,1:T(4,128)S(1)} %copy.205) | copy-start | bytes 580

commit v2 on v1

--- a/solution.py
+++ b/solution.py
@@ -445,6 +445,431 @@
     )(grads, block_out, input_gradient)
 
 
+def spread(count, slots, lead):
+    return [min(slots - 1, lead + (e * (slots - lead)) // count) for e in range(count)]
+
+
+def step_kernel(sizes, length, heads, head, slab_ref, x_ref, cot_ref, out_ref, y_ref, gx_ref,
+                buf, whi, wlo, xs, cots, fo_hi, fo_lo, so_hi, so_lo, cot_hi, cot_lo, gm_hi, gm_lo,
+                mixed, probs_hi, probs_lo, joined, mid, back, yb, staged, vec_ref, bias_ref, hidden_bias, small_grads,
+                swapped, landed, send_sem, recv_sem, swap_send, swap_recv,
+                push_send, push_recv, trade_send, trade_recv, stage_sem, image_sem, image_send, image_recv):
+    core, at = place(sizes)
+    number = functools.partial(slab_id, sizes=sizes)
+    n = sizes[0] * sizes[1] * sizes[2]
+    own, rows, width = xs.shape
+    share = slab_ref.shape[0]
+    hidden_local = hidden_bias.shape[-1]
+    qkv, attn = 5 * LANES, 6 * LANES
+    small, up = attn, attn + LANES
+    down, end = up + hidden_local, up + 2 * hidden_local
+    spans = ((0, up), (up, end))
+    partner = {"mp": 1 - core}
+
+    def block(slab, sign, of):
+        return pl.ds(pl.multiple_of(at(slab, sign, of) * share, 8), share)
+
+    def span(p):
+        return slice(*spans[p])
+
+    def landing(p, slab, of):
+        return buf.at[of, block(slab, -1, of), span(p)]
+
+    def gather_event(p, slab):
+        spot = landing(p, slab, core)
+        if any(slab):
+            pltpu.make_async_remote_copy(
+                src_ref=spot, dst_ref=spot, send_sem=send_sem.at[p, 0, 0], recv_sem=recv_sem.at[p, number(slab)],
+                device_id=partner).wait_recv()
+        source = spot if any(slab) else slab_ref.at[:, span(p)]
+        for r in reversed(sends(slab, sizes)):
+            pltpu.make_async_remote_copy(
+                src_ref=source, dst_ref=spot, send_sem=send_sem.at[p, r, number(slab)],
+                recv_sem=recv_sem.at[p, number(plus(slab, UNITS[r]))], device_id={"dp": at(UNITS[r])}).start()
+        pltpu.make_async_remote_copy(
+            src_ref=source, dst_ref=spot, send_sem=swap_send.at[p, number(slab)],
+            recv_sem=swap_recv.at[p, number(slab)], device_id=partner).start()
+
+    def gather_end(p):
+        for slab in order:
+            spot = landing(p, slab, 1 - core)
+            pltpu.make_async_remote_copy(
+                src_ref=spot, dst_ref=spot, send_sem=swap_send.at[p, 0], recv_sem=swap_recv.at[p, number(slab)],
+                device_id=partner).wait_recv()
+        for slab in order:
+            spot = landing(p, slab, core)
+            for r in sends(slab, sizes):
+                pltpu.make_async_remote_copy(
+                    src_ref=spot, dst_ref=spot, send_sem=send_sem.at[p, r, number(slab)],
+                    recv_sem=recv_sem.at[p, 0], device_id=partner).wait_send()
+            pltpu.make_async_remote_copy(
+                src_ref=spot, dst_ref=spot, send_sem=swap_send.at[p, number(slab)], recv_sem=swap_recv.at[p, 0],
+                device_id=partner).wait_send()
+
+    order = arrival_order(sizes)
+
+    first_size, side_size, _ = sizes
+    back_order = [(i, j, k) for k in reversed(range(side_size)) for j in reversed(range(side_size))
+                  for i in reversed(range(first_size))]
+
+    def trade(p, slab):
+        s = number(slab)
+        return pltpu.make_async_remote_copy(
+            src_ref=buf.at[1 - core, block(slab, 1, 1 - core), span(p)], dst_ref=swapped.at[s, :, span(p)],
+            send_sem=trade_send.at[p, s], recv_sem=trade_recv.at[p, s], device_id=partner)
+
+    def scatter_start(p):
+        for slab in back_order:
+            trade(p, slab).start()
+
+    def arrived(buffer, spot, p, sem):
+        ref = buffer.at[spot, :, span(p)]
+        pltpu.make_async_remote_copy(
+            src_ref=ref, dst_ref=ref, send_sem=trade_send.at[p, 0], recv_sem=sem, device_id=partner).wait_recv()
+        return ref[...]
+
+    def push(p, slab):
+        s = number(slab)
+        r = max(q for q in range(3) if slab[q])
+        return pltpu.make_async_remote_copy(
+            src_ref=buf.at[core, block(slab, 1, core), span(p)], dst_ref=landed.at[s - 1, :, span(p)],
+            send_sem=push_send.at[p, s], recv_sem=push_recv.at[p, s], device_id={"dp": at(UNITS[r])})
+
+    def scatter_event(p, slab):
+        s = number(slab)
+        here = (core, block(slab, 1, core), span(p))
+        value = buf[here] + arrived(swapped, s, p, trade_recv.at[p, s])
+        for r in range(3):
+            if not any(slab[r + 1:]) and slab[r] + 1 < sizes[r]:
+                spot = number(plus(slab, UNITS[r]))
+                value = value + arrived(landed, spot - 1, p, push_recv.at[p, spot])
+        if any(slab):
+            buf[here] = value
+            push(p, slab).start()
+        else:
+            out_ref[:, span(p)] = value
+
+    def scatter_end(p):
+        for slab in back_order:
+            trade(p, slab).wait_send()
+            if any(slab):
+                push(p, slab).wait_send()
+
+    def image_copies(t, source, ref, i):
+        spot = ref.at[core * own + i]
+        keep = pltpu.make_async_copy(source.at[i], spot, image_sem.at[t, i])
+        give = pltpu.make_async_remote_copy(
+            src_ref=source.at[i], dst_ref=spot, send_sem=image_send.at[t, i], recv_sem=image_recv.at[t, i],
+            device_id=partner)
+        theirs = ref.at[(1 - core) * own + i]
+        take = pltpu.make_async_remote_copy(
+            src_ref=theirs, dst_ref=theirs, send_sem=image_send.at[t, i], recv_sem=image_recv.at[t, i],
+            device_id=partner)
+        return keep, give, take
+
+    def weight(c, lo, hi):
+        return whi[c, :, lo:hi], wlo[c, :, lo:hi]
+
+    def vec(r):
+        return vec_ref[r:r + 1, :]
+
+    def normalize(v):
+        center = v - jnp.mean(v, axis=-1, keepdims=True)
+        inverse = lax.rsqrt(jnp.mean(center * center, axis=-1, keepdims=True) + norm_eps)
+        return center * inverse, inverse
+
+    def norm_back(grad, normed, inverse, gain):
+        scaled = grad * gain
+        return inverse * (scaled - jnp.mean(scaled, axis=-1, keepdims=True)
+                          - normed * jnp.mean(scaled * normed, axis=-1, keepdims=True))
+
+    def total(v):
+        return jnp.sum(v, axis=0, keepdims=True)
+
+    def convert(lo, hi):
+        def body(t, _):
+            c, r = t // (width // 16), t % (width // 16)
+            here = pl.ds(pl.multiple_of(r * 16, 16), 16)
+            high, low = split(buf[c, here, lo:hi])
+            whi[c, here, lo:hi] = high
+            wlo[c, here, lo:hi] = low
+            buf[c, here, lo:hi] = jnp.zeros((16, hi - lo), f32)
+            return 0
+
+        lax.fori_loop(0, 2 * (width // 16), body, 0)
+
+    def thirds(v):
+        high = v.astype(bf16)
+        v = v - high.astype(f32)
+        middle_term = v.astype(bf16)
+        return high, middle_term, (v - middle_term.astype(f32)).astype(bf16)
+
+    def moved(v, onehot, dim):
+        return sum(dot(term, onehot, 1, dim) for term in reversed(thirds(v)))
+
+    piece = head // n
+    entry = lax.broadcasted_iota(jnp.int32, (width, LANES), 0)
+    owner, inner = entry // share, entry % share
+    target = lax.broadcasted_iota(jnp.int32, (width, LANES), 1)
+
+    def attention_bias_at(t):
+        kind, which = inner // (heads * piece), (inner // piece) % heads
+        window = jnp.where(kind == 0, jnp.where(which < 2, 0, 3), jnp.where(which < 2, 2, 4))
+        place_in = (which % 2) * head + owner * piece + inner % piece
+        return ((window == t) & (place_in == target)).astype(f32).astype(bf16)
+
+    def hidden_bias_at(half, t):
+        flat = inner + half * share
+        place_in = (flat // piece) * head + owner * piece + flat % piece
+        return (place_in == target + t * LANES).astype(f32).astype(bf16)
+
+    greet(core, at, -1)
+    gather_event(0, (0, 0, 0))
+    staging = []
+    tiles = width // LANES
+    for t in range(tiles):
+        staging.append(pltpu.make_async_copy(x_ref.at[:, t * LANES:(t + 1) * LANES], staged.at[t], stage_sem.at[t]))
+        staging[-1].start()
+    buf[core, block((0, 0, 0), 1, core), :] = slab_ref[...]
+    xs[...] = jnp.zeros_like(xs)
+    cots[...] = jnp.zeros_like(cots)
+    small_grads[...] = jnp.zeros_like(small_grads)
+    for source, sink in ((x_ref, xs), (cot_ref, cots)):
+        for t in range(tiles):
+            lanes = slice(t * LANES, (t + 1) * LANES)
+            copy = pltpu.make_async_copy(source.at[:, lanes], staged.at[t], stage_sem.at[t])
+            if sink is cots:
+                copy.start()
+            copy.wait()
+            for i in range(own):
+                sink[i, 0:length, lanes] = staged[t, pl.ds(core * own + i, length, stride=2 * own), :]
+
+    for slab in order[1:]:
+        gather_event(0, slab)
+    gather_event(1, (0, 0, 0))
+    for i in range(own):
+        cot_hi[i], cot_lo[i] = split(cots[i])
+    gather_end(0)
+    for c in range(2):
+        turned = buf[c, :, small:up].T
+        if c == 0:
+            vec_ref[...] = turned[0:8, :]
+        packed = turned[0:16, :]
+        for t in range(5):
+            bias_ref[c, :, t * LANES:(t + 1) * LANES] = moved(packed[6:7], attention_bias_at(t), 0)
+        for t in range(hidden_local // LANES):
+            hidden_bias[c, :, t * LANES:(t + 1) * LANES] = (
+                moved(packed[7:8], hidden_bias_at(0, t), 0) + moved(packed[8:9], hidden_bias_at(1, t), 0))
+    convert(0, attn)
+
+    lane = lax.broadcasted_iota(jnp.int32, (rows, LANES), 1)
+    sides = (lane < head, lane >= head)
+    column = lax.broadcasted_iota(jnp.int32, (rows, rows), 1)
+    score_scale = head ** (-0.5)
+
+    def side(v, s):
+        return jnp.where(sides[s], v, 0.0)
+
+    def swap(v):
+        return pltpu.roll(v, head, 1)
+
+    def windows(i, c):
+        w = [mixed[i, c, :, t * LANES:(t + 1) * LANES] for t in range(5)]
+        return [
+            (side(w[0], 0) * score_scale, side(w[1], 0), side(w[2], 0)),
+            (side(w[0], 1) * score_scale, side(w[1], 1), side(w[2], 1)),
+            (side(w[3], 0) * score_scale, side(swap(w[3]), 0), side(w[4], 0)),
+        ]
+
+    def serve(t, h, plan, event):
+        for slot, slab in plan:
+            if slot % heads == h:
+                pl.when(t == slot // heads)(functools.partial(event, 1, slab))
+
+    gather_plan = list(zip(spread(len(order) - 1, 2 * own * heads, 1), order[1:]))
+
+    def attend(t, _):
+        i, c = t // 2, t % 2
+
+        @pl.when(c == 0)
+        def _():
+            normed, _ = normalize(xs[i])
+            fo_hi[i], fo_lo[i] = split(normed * vec(0) + vec(1))
+            mid[i] = xs[i] + vec(2)
+
+        mixed[i, c] = product((fo_hi[i], fo_lo[i]), weight(c, 0, qkv), 1, 0) + bias_ref[c]
+        outs = []
+        for h, (q, k, v) in enumerate(windows(i, c)):
+            serve(t, h, gather_plan, gather_event)
+            scores = product(split(q), split(k), 1, 1)
+            scores = jnp.where(column < length, scores, MASKED)
+            expon = jnp.exp(scores - jnp.max(scores, axis=-1, keepdims=True))
+            probs = split(expon / jnp.sum(expon, axis=-1, keepdims=True))
+            probs_hi[i, c, h], probs_lo[i, c, h] = probs
+            outs.append(product_apart(probs, split(v), 1, 0))
+        joined[i, c] = jnp.concatenate([swap(outs[2]), outs[0] + outs[1]], axis=1)
+        mid[i] += product(split(joined[i, c]), weight(c, 4 * LANES, attn), 1, 1)
+        return 0
+
+    lax.fori_loop(0, 2 * own, attend, 0)
+    gather_end(1)
+    convert(up, end)
+
+    def feed(t, _):
+        i, c = t // 2, t % 2
+
+        @pl.when(c == 0)
+        def _():
+            second, _ = normalize(mid[i])
+            so_hi[i], so_lo[i] = split(second * vec(3) + vec(4))
+            yb[i] = mid[i] + vec(5)
+            back[i] = jnp.zeros((rows, width), f32)
+
+        so = (so_hi[i], so_lo[i])
+        co = (cot_hi[i], cot_lo[i])
+        hidden = product(so, weight(c, up, down), 1, 0) + hidden_bias[c]
+        portion = 0.5 * (1.0 + lax.erf(hidden * (0.5 ** 0.5)))
+        active = split(hidden * portion)
+        slope = portion + hidden * jnp.exp(-0.5 * hidden * hidden) * 0.3989422804014327
+        yb[i] += product(active, weight(c, down, end), 1, 1)
+        buf[c, :, down:end] += product(co, active, 0, 0)
+        grad = product(co, weight(c, down, end), 1, 0) * slope
+        small_grads[c, 7:8, 0:hidden_local] += total(grad)
+        grad = split(grad)
+        buf[c, :, up:down] += product(so, grad, 0, 0)
+        back[i] += product(grad, weight(c, up, down), 1, 1)
+
+        @pl.when(c == 1)
+        def _():
+            cot = cots[i]
+            second, second_inverse = normalize(mid[i])
+            grad_second = back[i]
+            small_grads[0, 3:4, 0:width] += total(grad_second * second)
+            small_grads[0, 4:5, 0:width] += total(grad_second)
+            small_grads[0, 5:6, 0:width] += total(cot)
+            grad_middle = cot + norm_back(grad_second, second, second_inverse, vec(3))
+            small_grads[0, 2:3, 0:width] += total(grad_middle)
+            gm_hi[i], gm_lo[i] = split(grad_middle)
+            back[i] = grad_middle
+            mid[i] = jnp.zeros((rows, width), f32)
+
+        return 0
+
+    lax.fori_loop(0, 2 * own, feed, 0)
+
+    scatter_start(1)
+    for i in range(own):
+        keep, give, _ = image_copies(0, yb, y_ref, i)
+        keep.start()
+        give.start()
+    scatter_plan = list(zip(spread(len(back_order), 2 * own * heads, 1), back_order))
+
+    def attend_back(t, _):
+        i, c = t // 2, t % 2
+        gm = (gm_hi[i], gm_lo[i])
+        fo = (fo_hi[i], fo_lo[i])
+        grad_heads = product(gm, weight(c, 4 * LANES, attn), 1, 0)
+        buf[c, :, 4 * LANES:attn] += product(gm, split(joined[i, c]), 0, 0)
+        pair, single = grad_heads[:, LANES:], swap(grad_heads[:, :LANES])
+        pair_out, single_out = joined[i, c, :, LANES:], swap(joined[i, c, :, :LANES])
+        grad_outs = (side(pair, 0), side(pair, 1), side(single, 0))
+        outs = (pair_out, pair_out, single_out)
+        grads = []
+        for h, (q, k, v) in enumerate(windows(i, c)):
+            serve(t, h, scatter_plan, scatter_event)
+            grad_out = grad_outs[h]
+            row = jnp.sum(grad_out * outs[h], axis=-1, keepdims=True)
+            grad_out = split(grad_out)
+            grad_probs = product(grad_out, split(v), 1, 1)
+            probs = (probs_hi[i, c, h], probs_lo[i, c, h])
+            grad_v = product(probs, grad_out, 0, 0)
+            grad_scores = split((probs[0].astype(f32) + probs[1].astype(f32)) * (grad_probs - row))
+            grad_q = product_apart(grad_scores, split(k), 1, 0) * score_scale
+            grad_k = product(grad_scores, split(q), 0, 0)
+            grads.append((grad_q, grad_k, grad_v))
+        one, two, three = grads
+        grad_mixed = jnp.concatenate(
+            [one[0] + two[0], one[1] + two[1], one[2] + two[2], three[0] + swap(three[1]), three[2]], axis=1)
+        small_grads[c, 6:7, 0:qkv] += total(grad_mixed)
+        grad_mixed = split(grad_mixed)
+        buf[c, :, 0:qkv] += product(fo, grad_mixed, 0, 0)
+        mid[i] += product(grad_mixed, weight(c, 0, qkv), 1, 1)
+
+        @pl.when(c == 1)
+        def _():
+            first, first_inverse = normalize(xs[i])
+            grad_first = mid[i]
+            small_grads[0, 0:1, 0:width] += total(grad_first * first)
+            small_grads[0, 1:2, 0:width] += total(grad_first)
+            xs[i] = back[i] + norm_back(grad_first, first, first_inverse, vec(0))
+
+        return 0
+
+    lax.fori_loop(0, 2 * own, attend_back, 0)
+
+    for c in range(2):
+        bias = sum(moved(small_grads[c, 6:7, t * LANES:(t + 1) * LANES], attention_bias_at(t), 1) for t in range(5))
+        hidden = [sum(moved(small_grads[c, 7:8, t * LANES:(t + 1) * LANES], hidden_bias_at(half, t), 1)
+                      for t in range(hidden_local // LANES)) for half in range(2)]
+        six = small_grads[0, 0:6, 0:width]
+        packed = jnp.concatenate([six, bias, hidden[0], hidden[1], jnp.zeros((LANES - 9, width), f32)], axis=0)
+        buf[c, :, small:up] = packed.T
+    scatter_start(0)
+    for i in range(own):
+        keep, give, _ = image_copies(1, xs, gx_ref, i)
+        keep.start()
+        give.start()
+    for slab in back_order:
+        scatter_event(0, slab)
+    for t, source, ref in ((0, yb, y_ref), (1, xs, gx_ref)):
+        for i in range(own):
+            keep, give, take = image_copies(t, source, ref, i)
+            keep.wait()
+            give.wait_send()
+            take.wait_recv()
+    scatter_end(1)
+    scatter_end(0)
+
+
+def run_step(slab, inputs, cotangent, n, heads, head, length):
+    sizes = rings(n)
+    width = inputs.shape[1]
+    images = inputs.shape[0] // length
+    own = images // 2
+    rows = -(-length // 16) * 16
+    share, columns = slab.shape
+    hidden_local = (columns - 7 * LANES) // 2
+    anywhere = pl.BlockSpec(memory_space=pl.ANY)
+    act = pltpu.VMEM((own, rows, width), bf16)
+    full = pltpu.VMEM((own, rows, width), f32)
+    dma = pltpu.SemaphoreType.DMA
+    probs = pltpu.VMEM((own, 2, heads, rows, rows), bf16)
+    return pl.pallas_call(
+        functools.partial(step_kernel, sizes, length, heads, head),
+        out_shape=[jax.ShapeDtypeStruct(slab.shape, f32), jax.ShapeDtypeStruct((images, rows, width), f32),
+                   jax.ShapeDtypeStruct((images, rows, width), f32)],
+        in_specs=[pl.BlockSpec(memory_space=pltpu.VMEM), anywhere, anywhere],
+        out_specs=[pl.BlockSpec(memory_space=pltpu.VMEM), anywhere, anywhere],
+        scratch_shapes=[
+            pltpu.VMEM((2, width, columns), f32),
+            pltpu.VMEM((2, width, columns), bf16), pltpu.VMEM((2, width, columns), bf16),
+            full, full, act, act, act, act, act, act, act, act,
+            pltpu.VMEM((own, 2, rows, 5 * LANES), f32), probs, probs,
+            pltpu.VMEM((own, 2, rows, 2 * LANES), f32), full, full, full,
+            pltpu.VMEM((width // LANES, inputs.shape[0], LANES), f32),
+            pltpu.VMEM((8, width), f32), pltpu.VMEM((2, 1, 5 * LANES), f32), pltpu.VMEM((2, 1, hidden_local), f32),
+            pltpu.VMEM((2, 8, hidden_local), f32),
+            pltpu.VMEM((n, share, columns), f32), pltpu.VMEM((n - 1, share, columns), f32),
+            dma((2, 3, n)), dma((2, n)), dma((2, n)), dma((2, n)),
+            dma((2, n)), dma((2, n)), dma((2, n)), dma((2, n)),
+            dma((width // LANES,)), dma((2, own)), dma((2, own)), dma((2, own)),
+        ],
+        compiler_params=pltpu.CompilerParams(
+            collective_id=2, has_side_effects=True, vmem_limit_bytes=67043328),
+        name="step",
+    )(slab, inputs, cotangent)
+
+
 def pack_attention(mixer, output):
     head = mixer.shape[2] // 3
     pair = 2 * head
@@ -495,6 +920,48 @@
 
 
 def per_device(inputs, cotangent, *rest):
+    if rest[0].shape[0] % 8 == 0:
+        return one_kernel(inputs, cotangent, *rest)
+    return three_kernels(inputs, cotangent, *rest)
+
+
+def finish(params, momenta, variances, gradients, block_out, input_gradient):
+    results = [adam_update(params[m], gradients[m], momenta[m], variances[m], weight_decay if m in DECAYED else 0.0)
+               for m in NAMES]
+    return (block_out, input_gradient, *(gradients[m] for m in NAMES), *(r[0] for r in results),
+            *(r[1] for r in results), *(r[2] for r in results))
+
+
+def one_kernel(inputs, cotangent, *rest):
+    n = lax.axis_size("dp")
+    images, length, width = inputs.shape
+    scale = (n * images * length) ** (-0.5)
+    params = dict(zip(NAMES, rest[:12]))
+    momenta = dict(zip(NAMES, rest[12:24]))
+    variances = dict(zip(NAMES, rest[24:]))
+    share = params["first_gain"].shape[0]
+    heads, piece = params["mixer_bias"].shape[1:]
+    head = piece * n
+    hidden_local = params["expand_weight"].shape[1]
+    small = jnp.pad(pack_small(params).reshape(-1, share).T, ((0, 0), (0, LANES - 9)))
+    slab = jnp.concatenate([
+        pack_attention(params["mixer_weight"], params["output_weight"]), small,
+        params["expand_weight"], params["reduce_weight"].T], axis=1)
+
+    def tokens(v):
+        return v.transpose(1, 0, 2).reshape(length * images, width)
+
+    summed, block_out, input_gradient = run_step(slab, tokens(inputs), tokens(cotangent), n, heads, head, length)
+    summed = summed * scale
+    mixer, output = unpack_attention(summed[:, :6 * LANES], head)
+    gradients = unpack_small(summed[:, 6 * LANES:6 * LANES + 9].T.reshape(-1), params)
+    up = 7 * LANES
+    gradients.update(mixer_weight=mixer, output_weight=output, expand_weight=summed[:, up:up + hidden_local],
+                     reduce_weight=summed[:, up + hidden_local:].T)
+    return finish(params, momenta, variances, gradients, block_out[:, :length], input_gradient[:, :length])
+
+
+def three_kernels(inputs, cotangent, *rest):
     n = lax.axis_size("dp")
     scale = (n * inputs.shape[0] * inputs.shape[1]) ** (-0.5)
     params = dict(zip(NAMES, rest[:12]))
@@ -529,8 +996,6 @@
     block_out, input_gradient, grads, small_grads = run_layer(
         base, inputs, cotangent, gathered.reshape(2, width, columns), vectors, mixed_bias, expand_bias, heads, head)
 
-    six = jnp.broadcast_to(small_grads[0, :6, :width].reshape(1, 6, n, share), (2, 6, n, share))
-    six = six * (jnp.arange(2) == 0).astype(f32).reshape(2, 1, 1, 1)
     total = small_grads[:1, :6, :width].reshape(6, n, share).transpose(1, 0, 2).reshape(n, 6 * share)
     row = small_grads[:, 6, :5 * LANES]
     bias = jnp.stack([
@@ -549,10 +1014,7 @@
     gradients.update(mixer_weight=mixer, output_weight=output,
                      expand_weight=summed[:, 6 * LANES:6 * LANES + hidden_local],
                      reduce_weight=summed[:, 6 * LANES + hidden_local:end].T)
-    results = [adam_update(params[m], gradients[m], momenta[m], variances[m], weight_decay if m in DECAYED else 0.0)
-               for m in NAMES]
-    return (block_out, input_gradient, *(gradients[m] for m in NAMES), *(r[0] for r in results),
-            *(r[1] for r in results), *(r[2] for r in results))
+    return finish(params, momenta, variances, gradients, block_out, input_gradient)
 
 
 def solution(mesh):

time: 201 us -> 187 us (0.930)
  local copies, waits for them, and re-layouts: 29.6 us -> 16.3 us
    unnamed x95 -> x99, local copies, waits for them, and re-layouts: 15.6 us -> 8.48 us
    pallas_call x3 -> x1, Pallas kernels: 165 us -> 164 us  [run_step(): pl.pallas_call(functools.partial(step_kernel, sizes, length, heads, head)...]
    sub x8 -> x9, other arithmetic: 4.73 us -> 5.15 us  [adam_update(): param - learn_rate * (mean_hat / (jnp.sqrt(square_hat) + adam_eps) + deca...]
where the time goes in v2:
time: 187 us
  Pallas kernels  164 us (88%)
  local copies, waits for them, and re-layouts  16.3 us (9%)
  other arithmetic  5.19 us (3%)
    pallas_call x1, Pallas kernels, run_step(): pl.pallas_call(functools.partial(step_kernel, sizes, length, heads, head)...  164 us
    unnamed x99, local copies, waits for them, and re-layouts  8.48 us
    sub x9, other arithmetic, adam_update(): param - learn_rate * (mean_hat / (jnp.sqrt(square_hat) + adam_eps) + deca...  5.15 us

profile of v2, /device:TPU:0, one launch (start us, length us, event | category | flops | bytes accessed | tf_op | source)
XLA Modules:
  0.0 186.7 jit_solution(13630994013663116580)
XLA Ops:
  0.7 0.8 slice_bitcast_fusion.1
  1.5 0.7 slice.181
  2.3 0.7 slice.182
  3.0 0.7 copy.131
  3.6 0.1 reshape.132
  3.7 0.8 copy.132
  4.5 0.1 reshape.133
  4.6 0.8 concatenate.22
  5.4 0.1 reshape.134
  5.5 0.1 copy.133
  5.6 1.7 concatenate.23.slab_ref
  7.3 163.7 %step.1 = (f32[24,2432]{1,0:T(8,128)}, f32[8,208,384]{2,1,0:T(8,128)}, f32[8,208,384]{2,1,0:T(8,128)}) custom-call(f32[24,2432]{1,0:T(8,128)} %concatenate.23.slab_ref, f32[1576,384]{1,0:T(8,128)} %bitcast.29, f32[1576,384]{1,0:T(8,128)} %bitcast.30), custom_call_target="tpu_custom_call" | custom-call | tf_op jit(solution)/shard_map/step/pallas_call | solution.py:847
  171.0 1.9 slice.148
  172.9 1.9 copy.142
  174.8 0.6 copy-done
  175.4 0.2 slice.149
  175.5 0.0 copy-start.1
  175.5 0.0 copy-start.6
  175.6 0.0 copy-start.7
  175.6 0.0 copy-start.5
  175.6 0.0 copy-start.12
  175.6 0.0 copy-start.13
  175.6 0.0 copy-start.2
  175.6 0.0 copy-start.8
  175.6 0.0 copy-start.9
  175.6 0.0 copy-start.3
  175.7 0.0 copy-start.10
  175.7 1.9 copy.143
  177.6 0.0 copy-start.35
  177.6 0.0 copy-start.36
  177.6 0.0 copy-start.18
  177.6 0.0 copy-start.27
  177.6 0.0 copy-start.37
  177.7 0.0 copy-start.38
  177.7 0.0 copy-start.29
  177.7 0.0 copy-start.30
  177.7 0.0 copy-start.43
  177.7 0.0 copy-start.44
  177.8 0.0 copy-start.32
  177.8 0.3 slice_reduce_fusion
  178.2 0.0 copy-start.20
  178.2 0.0 copy-start.21
  178.2 0.0 copy-start.22
  178.2 0.0 copy-start.23
  178.2 0.0 copy-start.24
  178.2 0.1 fusion.27
  178.4 0.8 multiply_subtract_fusion.2
  179.1 0.1 reshape.137
  179.2 0.6 copy.144
  179.8 0.6 multiply_subtract_fusion.3
  180.5 0.7 multiply_subtract_fusion.1
  181.2 0.1 slice.199
  181.3 0.1 copy.134
  181.3 0.1 reshape.138
  181.4 0.1 copy.145
  181.5 0.0 copy-start.16
  181.5 0.8 multiply_subtract_fusion
  182.3 0.5 multiply_subtract_fusion.10
  182.9 0.6 copy.146
  183.5 0.5 multiply_subtract_fusion.8
  184.1 0.5 multiply_subtract_fusion.6
  184.7 0.6 multiply_subtract_fusion.5
  185.3 0.6 copy.147
  185.9 0.6 copy.148
  (74 shorter events, 0.2 us)
Async XLA Ops:
  172.9 2.5 %copy-start = (f32[8,208,384]{2,1,0:T(8,128)S(1)}, f32[8,208,384]{2,1,0:T(8,128)}, u32[]{:S(2)}) copy-start(f32[8,208,384]{2,1,0:T(8,128)} %get-tuple-element.54) | copy-start | bytes 7667716
  175.5 2.3 %copy-start.4 = (f32[24,2432]{1,0:T(8,128)S(1)}, f32[24,2432]{1,0:T(8,128)}, u32[]{:S(2)}) copy-start(f32[24,2432]{1,0:T(8,128)} %get-tuple-element.55) | copy-start | bytes 700420
  175.5 2.8 %copy-start.1 = (f32[24,3,192]{2,0,1:T(8,128)S(1)}, f32[24,3,192]{2,0,1:T(8,128)}, u32[]{:S(2)}) copy-start(f32[24,3,192]{2,0,1:T(8,128)} %param.42) | copy-start | bytes 165892
  175.5 2.8 %copy-start.6 = (f32[24,3,192]{2,0,1:T(8,128)S(1)}, f32[24,3,192]{2,0,1:T(8,128)}, u32[]{:S(2)}) copy-start(f32[24,3,192]{2,0,1:T(8,128)} %param.54) | copy-start | bytes 165892
  175.6 2.8 %copy-start.7 = (f32[24,3,192]{2,0,1:T(8,128)S(1)}, f32[24,3,192]{2,0,1:T(8,128)}, u32[]{:S(2)}) copy-start(f32[24,3,192]{2,0,1:T(8,128)} %param.66) | copy-start | bytes 165892
  175.6 4.2 %copy-start.5 = (f32[192,24]{0,1:T(8,128)S(1)}, f32[192,24]{0,1:T(8,128)}, u32[]{:S(2)}) copy-start(f32[192,24]{0,1:T(8,128)} %param.44) | copy-start | bytes 55300
  175.6 4.2 %copy-start.12 = (f32[192,24]{0,1:T(8,128)S(1)}, f32[192,24]{0,1:T(8,128)}, u32[]{:S(2)}) copy-start(f32[192,24]{0,1:T(8,128)} %param.56) | copy-start | bytes 55300
  175.6 4.2 %copy-start.13 = (f32[192,24]{0,1:T(8,128)S(1)}, f32[192,24]{0,1:T(8,128)}, u32[]{:S(2)}) copy-start(f32[192,24]{0,1:T(8,128)} %param.68) | copy-start | bytes 55300
  175.6 4.8 %copy-start.2 = (f32[24,768]{1,0:T(8,128)S(1)}, f32[24,768]{1,0:T(8,128)}, u32[]{:S(2)}) copy-start(f32[24,768]{1,0:T(8,128)} %param.48) | copy-start | bytes 221188
  175.6 4.8 %copy-start.8 = (f32[24,768]{1,0:T(8,128)S(1)}, f32[24,768]{1,0:T(8,128)}, u32[]{:S(2)}) copy-start(f32[24,768]{1,0:T(8,128)} %param.60) | copy-start | bytes 221188
  175.6 4.8 %copy-start.9 = (f32[24,768]{1,0:T(8,128)S(1)}, f32[24,768]{1,0:T(8,128)}, u32[]{:S(2)}) copy-start(f32[24,768]{1,0:T(8,128)} %param.72) | copy-start | bytes 221188
  175.6 5.9 %copy-start.3 = (f32[768,24]{0,1:T(8,128)S(1)}, f32[768,24]{0,1:T(8,128)}, u32[]{:S(2)}) copy-start(f32[768,24]{0,1:T(8,128)} %param.50) | copy-start | bytes 221188
  175.7 5.9 %copy-start.10 = (f32[768,24]{0,1:T(8,128)S(1)}, f32[768,24]{0,1:T(8,128)}, u32[]{:S(2)}) copy-start(f32[768,24]{0,1:T(8,128)} %param.62) | copy-start | bytes 221188
  175.7 5.8 %copy-start.11 = (f32[768,24]{0,1:T(8,128)S(1)}, f32[768,24]{0,1:T(8,128)}, u32[]{:S(2)}) copy-start(f32[768,24]{0,1:T(8,128)} %param.74) | copy-start | bytes 221188
  177.5 4.7 %copy-start.25 = (f32[24]{0:T(128)S(1)}, f32[24]{0:T(128)}, u32[]{:S(2)}) copy-start(f32[24]{0:T(128)} %param.40) | copy-start | bytes 292
  177.5 4.7 %copy-start.26 = (f32[24]{0:T(128)S(1)}, f32[24]{0:T(128)}, u32[]{:S(2)}) copy-start(f32[24]{0:T(128)} %param.41) | copy-start | bytes 292
  177.5 4.7 %copy-start.33 = (f32[24]{0:T(128)S(1)}, f32[24]{0:T(128)}, u32[]{:S(2)}) copy-start(f32[24]{0:T(128)} %param.53) | copy-start | bytes 292
  177.6 4.8 %copy-start.34 = (f32[24]{0:T(128)S(1)}, f32[24]{0:T(128)}, u32[]{:S(2)}) copy-start(f32[24]{0:T(128)} %param.65) | copy-start | bytes 292
  177.6 4.8 %copy-start.35 = (f32[24]{0:T(128)S(1)}, f32[24]{0:T(128)}, u32[]{:S(2)}) copy-start(f32[24]{0:T(128)} %param.64) | copy-start | bytes 292
  177.6 4.8 %copy-start.36 = (f32[24]{0:T(128)S(1)}, f32[24]{0:T(128)}, u32[]{:S(2)}) copy-start(f32[24]{0:T(128)} %param.52) | copy-start | bytes 292
  177.6 5.3 %copy-start.14 = (f32[2,3,4]{2,0,1:T(2,128)S(1)}, f32[2,3,4]{2,0,1:T(2,128)}, u32[]{:S(2)}) copy-start(f32[2,3,4]{2,0,1:T(2,128)} %param.43) | copy-start | bytes 292
  177.6 5.3 %copy-start.17 = (f32[2,3,4]{2,0,1:T(2,128)S(1)}, f32[2,3,4]{2,0,1:T(2,128)}, u32[]{:S(2)}) copy-start(f32[2,3,4]{2,0,1:T(2,128)} %param.55) | copy-start | bytes 292
  177.6 5.3 %copy-start.18 = (f32[2,3,4]{2,0,1:T(2,128)S(1)}, f32[2,3,4]{2,0,1:T(2,128)}, u32[]{:S(2)}) copy-start(f32[2,3,4]{2,0,1:T(2,128)} %param.67) | copy-start | bytes 292
  177.6 5.9 %copy-start.27 = (f32[24]{0:T(128)S(1)}, f32[24]{0:T(128)}, u32[]{:S(2)}) copy-start(f32[24]{0:T(128)} %param.45) | copy-start | bytes 292
  177.6 5.9 %copy-start.28 = (f32[24]{0:T(128)S(1)}, f32[24]{0:T(128)}, u32[]{:S(2)}) copy-start(f32[24]{0:T(128)} %param.46) | copy-start | bytes 292
  177.6 5.9 %copy-start.37 = (f32[24]{0:T(128)S(1)}, f32[24]{0:T(128)}, u32[]{:S(2)}) copy-start(f32[24]{0:T(128)} %param.58) | copy-start | bytes 292
  177.7 5.9 %copy-start.38 = (f32[24]{0:T(128)S(1)}, f32[24]{0:T(128)}, u32[]{:S(2)}) copy-start(f32[24]{0:T(128)} %param.70) | copy-start | bytes 292
  177.7 5.9 %copy-start.39 = (f32[24]{0:T(128)S(1)}, f32[24]{0:T(128)}, u32[]{:S(2)}) copy-start(f32[24]{0:T(128)} %param.69) | copy-start | bytes 292
  177.7 5.9 %copy-start.40 = (f32[24]{0:T(128)S(1)}, f32[24]{0:T(128)}, u32[]{:S(2)}) copy-start(f32[24]{0:T(128)} %param.57) | copy-start | bytes 292
  177.7 6.4 %copy-start.29 = (f32[24]{0:T(128)S(1)}, f32[24]{0:T(128)}, u32[]{:S(2)}) copy-start(f32[24]{0:T(128)} %param.47) | copy-start | bytes 292
  177.7 6.4 %copy-start.30 = (f32[24]{0:T(128)S(1)}, f32[24]{0:T(128)}, u32[]{:S(2)}) copy-start(f32[24]{0:T(128)} %param.51) | copy-start | bytes 292
  177.7 6.4 %copy-start.41 = (f32[24]{0:T(128)S(1)}, f32[24]{0:T(128)}, u32[]{:S(2)}) copy-start(f32[24]{0:T(128)} %param.63) | copy-start | bytes 292
  177.7 6.4 %copy-start.42 = (f32[24]{0:T(128)S(1)}, f32[24]{0:T(128)}, u32[]{:S(2)}) copy-start(f32[24]{0:T(128)} %param.75) | copy-start | bytes 292
  177.7 6.4 %copy-start.43 = (f32[24]{0:T(128)S(1)}, f32[24]{0:T(128)}, u32[]{:S(2)}) copy-start(f32[24]{0:T(128)} %param.71) | copy-start | bytes 292
  177.7 6.4 %copy-start.44 = (f32[24]{0:T(128)S(1)}, f32[24]{0:T(128)}, u32[]{:S(2)}) copy-start(f32[24]{0:T(128)} %param.59) | copy-start | bytes 292
  177.8 6.9 %copy-start.15 = (f32[12,4]{0,1:T(4,128)S(1)}, f32[12,4]{0,1:T(4,128)}, u32[]{:S(2)}) copy-start(f32[12,4]{0,1:T(4,128)} %param.49) | copy-start | bytes 580
  177.8 6.9 %copy-start.31 = (f32[12,4]{0,1:T(4,128)S(1)}, f32[12,4]{0,1:T(4,128)}, u32[]{:S(2)}) copy-start(f32[12,4]{0,1:T(4,128)} %param.61) | copy-start | bytes 580
  177.8 6.9 %copy-start.32 = (f32[12,4]{0,1:T(4,128)S(1)}, f32[12,4]{0,1:T(4,128)}, u32[]{:S(2)}) copy-start(f32[12,4]{0,1:T(4,128)} %param.73) | copy-start | bytes 580
  178.1 8.3 %copy-start.19 = (f32[24]{0:T(128)}, f32[24]{0:T(128)S(1)}, u32[]{:S(2)}) copy-start(f32[24]{0:T(128)S(1)} %get-tuple-element.206) | copy-start | bytes 292
  178.2 8.3 %copy-start.20 = (f32[24]{0:T(128)}, f32[24]{0:T(128)S(1)}, u32[]{:S(2)}) copy-start(f32[24]{0:T(128)S(1)} %get-tuple-element.207) | copy-start | bytes 292
  178.2 8.3 %copy-start.21 = (f32[24]{0:T(128)}, f32[24]{0:T(128)S(1)}, u32[]{:S(2)}) copy-start(f32[24]{0:T(128)S(1)} %get-tuple-element.208) | copy-start | bytes 292
  178.2 8.3 %copy-start.22 = (f32[24]{0:T(128)}, f32[24]{0:T(128)S(1)}, u32[]{:S(2)}) copy-start(f32[24]{0:T(128)S(1)} %get-tuple-element.209) | copy-start | bytes 292
  178.2 8.3 %copy-start.23 = (f32[24]{0:T(128)}, f32[24]{0:T(128)S(1)}, u32[]{:S(2)}) copy-start(f32[24]{0:T(128)S(1)} %get-tuple-element.211) | copy-start | bytes 292
  178.2 8.3 %copy-start.24 = (f32[24]{0:T(128)}, f32[24]{0:T(128)S(1)}, u32[]{:S(2)}) copy-start(f32[24]{0:T(128)S(1)} %get-tuple-element.212) | copy-start | bytes 292
  181.5 5.0 %copy-start.16 = (f32[12,4]{0,1:T(4,128)}, f32[12,4]{0,1:T(4,128)S(1)}, u32[]{:S(2)}) copy-start(f32[12,4]{0,1:T(4,128)S(1)} %copy.145) | copy-start | bytes 580

commit v3 on v2

--- a/solution.py
+++ b/solution.py
@@ -37,7 +37,9 @@
 
 
 def product_apart(a, b, da, db):
-    return dot(a[0], b[0], da, db) + dot(a[0], b[1], da, db) + dot(a[1], b[0], da, db)
+    n = b[0].shape[1 - db]
+    both = dot(a[0], jnp.concatenate(b, axis=1 - db), da, db)
+    return both[:, :n] + both[:, n:] + dot(a[1], b[0], da, db)
 
 
 def layer_kernel(length, heads, head, base, x_ref, cot_ref, w_ref, vec_ref, mb_ref, eb_ref,
@@ -188,10 +190,10 @@
             grad_out = split(grad_out)
             grad_probs = product(grad_out, split(v), 1, 1)
             probs = (probs_hi[c, h], probs_lo[c, h])
-            grad_v = product(probs, grad_out, 0, 0)
+            grad_v = product_apart(probs, grad_out, 0, 0)
             grad_scores = split((probs[0].astype(f32) + probs[1].astype(f32)) * (grad_probs - row))
             grad_q = product_apart(grad_scores, split(k), 1, 0) * score_scale
-            grad_k = product(grad_scores, split(q), 0, 0)
+            grad_k = product_apart(grad_scores, split(q), 0, 0)
             grads.append((grad_q, grad_k, grad_v))
         one, two, three = grads
         grad_mixed = jnp.concatenate(
@@ -259,14 +261,24 @@
 def place(sizes):
     first, side, _ = sizes
     core, me = lax.axis_index("mp"), lax.axis_index("dp")
-    a, b, c = me // (side * side), (me // side) % side, me % side
-
-    def at(slab, sign=1, of=core):
+    a, b, c = lax.div(me, side * side), lax.rem(lax.div(me, side), side), lax.rem(me, side)
+    firsts = [lax.rem(a + i, first) * (side * side) for i in range(first)]
+    bs = [lax.rem(b + j, side) for j in range(side)]
+    cs = [lax.rem(c + j, side) for j in range(side)]
+    cores = {"mine": core, "other": 1 - core}
+    pairs = {}
+    for of, which in cores.items():
+        for j in range(side):
+            for k in range(side):
+                ahead_b = bs[j] * which + bs[k] * (1 - which)
+                ahead_c = cs[k] * which + cs[j] * (1 - which)
+                pairs[of, j, k] = ahead_b * side + ahead_c
+    places = {(of, i, j, k): firsts[i] + pairs[of, j, k]
+              for of in cores for i in range(first) for j in range(side) for k in range(side)}
+
+    def at(slab, sign=1, of="mine"):
         i, j, k = slab
-        i, j, k = (sign * i) % first, (sign * j) % side, (sign * k) % side
-        ahead_b = j * of + k * (1 - of)
-        ahead_c = k * of + j * (1 - of)
-        return (((a + i) % first) * side + (b + ahead_b) % side) * side + (c + ahead_c) % side
+        return places[of, (sign * i) % first, (sign * j) % side, (sign * k) % side]
 
     return core, at
 
@@ -279,7 +291,24 @@
 
 
 def sends(slab, sizes):
-    return [r for r in range(3) if not any(slab[r + 1:]) and slab[r] + 1 < sizes[r]]
+    out = [(0, (i, 0, 0), (i, 0, 0)) for i in range(1, sizes[0])] if not any(slab) else []
+    for r in (1, 2):
+        if not any(slab[r + 1:]) and slab[r] + 1 < sizes[r]:
+            out.append((r, UNITS[r], plus(slab, UNITS[r])))
+    return out
+
+
+def sources(slab, sizes):
+    out = [(i, 0, 0) for i in range(1, sizes[0])] if not any(slab) else []
+    for r in (1, 2):
+        if not any(slab[r + 1:]) and slab[r] + 1 < sizes[r]:
+            out.append(plus(slab, UNITS[r]))
+    return out
+
+
+def hop(slab):
+    r = max(q for q in range(3) if slab[q])
+    return slab if r == 0 else UNITS[r]
 
 
 def arrival_order(sizes):
@@ -287,9 +316,9 @@
     while heap:
         now, slab = heapq.heappop(heap)
         order.append(slab)
-        for r in sends(slab, sizes):
+        for r, _, there in sends(slab, sizes):
             free[r] = max(now, free[r]) + cost[r]
-            heapq.heappush(heap, (free[r], plus(slab, UNITS[r])))
+            heapq.heappush(heap, (free[r] + 1.0, there))
     return order
 
 
@@ -297,35 +326,36 @@
     return (slab[0] * sizes[1] + slab[1]) * sizes[2] + slab[2]
 
 
-def greet(core, at, sign):
+def greet(core, at, sizes):
     barrier = pltpu.get_barrier_semaphore()
-    for unit in UNITS:
-        pl.semaphore_signal(barrier, inc=1, device_id={"dp": at(unit, sign)})
+    backs = [(i, 0, 0) for i in range(1, sizes[0])] + [UNITS[1], UNITS[2]]
+    for steps in backs:
+        pl.semaphore_signal(barrier, inc=1, device_id={"dp": at(steps, -1)})
     pl.semaphore_signal(barrier, inc=1, device_id={"mp": 1 - core})
-    pl.semaphore_wait(barrier, 4)
+    pl.semaphore_wait(barrier, len(backs) + 1)
 
 
 def gather_kernel(sizes, slab_ref, out_ref, send_sem, recv_sem, swap_send, swap_recv, own_sem):
     core, at = place(sizes)
     number = functools.partial(slab_id, sizes=sizes)
-    greet(core, at, -1)
+    greet(core, at, sizes)
 
     def landing(slab, of):
-        return out_ref.at[of, at(slab, -1, of)]
+        return out_ref.at[core if of == "mine" else 1 - core, at(slab, -1, of)]
 
     started = []
-    own = pltpu.make_async_copy(slab_ref, landing((0, 0, 0), core), own_sem)
+    own = pltpu.make_async_copy(slab_ref, landing((0, 0, 0), "mine"), own_sem)
     for slab in arrival_order(sizes):
-        spot = landing(slab, core)
+        spot = landing(slab, "mine")
         if any(slab):
             pltpu.make_async_remote_copy(
                 src_ref=spot, dst_ref=spot, send_sem=send_sem.at[0, 0], recv_sem=recv_sem.at[number(slab)],
                 device_id={"mp": 1 - core}).wait_recv()
         source = spot if any(slab) else slab_ref
-        for r in reversed(sends(slab, sizes)):
+        for r, steps, there in reversed(sends(slab, sizes)):
             copy = pltpu.make_async_remote_copy(
-                src_ref=source, dst_ref=spot, send_sem=send_sem.at[r, number(slab)],
-                recv_sem=recv_sem.at[number(plus(slab, UNITS[r]))], device_id={"dp": at(UNITS[r])})
+                src_ref=source, dst_ref=spot, send_sem=send_sem.at[r, number(there)],
+                recv_sem=recv_sem.at[number(there)], device_id={"dp": at(steps)})
             copy.start()
             started.append(copy)
         copy = pltpu.make_async_remote_copy(
@@ -336,7 +366,7 @@
         if not any(slab):
             own.start()
     for slab in arrival_order(sizes):
-        spot = landing(slab, 1 - core)
+        spot = landing(slab, "other")
         pltpu.make_async_remote_copy(
             src_ref=spot, dst_ref=spot, send_sem=swap_send.at[0], recv_sem=swap_recv.at[number(slab)],
             device_id={"mp": 1 - core}).wait_recv()
@@ -366,7 +396,7 @@
     del y_in, gx_in
     core, at = place(sizes)
     number = functools.partial(slab_id, sizes=sizes)
-    greet(core, at, -1)
+    greet(core, at, sizes)
     first, side, _ = sizes
     order = [(i, j, k) for k in reversed(range(side)) for j in reversed(range(side)) for i in reversed(range(first))]
     own = y_ref.shape[0] // 2
@@ -374,7 +404,7 @@
     for slab in order:
         s = number(slab)
         copy = pltpu.make_async_remote_copy(
-            src_ref=g_ref.at[1 - core, at(slab, 1, 1 - core)], dst_ref=swapped.at[s],
+            src_ref=g_ref.at[1 - core, at(slab, 1, "other")], dst_ref=swapped.at[s],
             send_sem=swap_send.at[s], recv_sem=swap_recv.at[s], device_id={"mp": 1 - core})
         copy.start()
         started.append(copy)
@@ -402,16 +432,14 @@
         s = number(slab)
         loads[slab].wait()
         value = acc[s] + arrived(swapped, s, swap_recv.at[s])
-        for r in range(3):
-            if not any(slab[r + 1:]) and slab[r] + 1 < sizes[r]:
-                spot = number(plus(slab, UNITS[r]))
-                value = value + arrived(landed, spot - 1, recv_sem.at[spot])
+        for other in sources(slab, sizes):
+            spot = number(other)
+            value = value + arrived(landed, spot - 1, recv_sem.at[spot])
         if any(slab):
             acc[s] = value
-            r = max(q for q in range(3) if slab[q])
             copy = pltpu.make_async_remote_copy(
                 src_ref=acc.at[s], dst_ref=landed.at[s - 1], send_sem=send_sem.at[s], recv_sem=recv_sem.at[s],
-                device_id={"dp": at(UNITS[r])})
+                device_id={"dp": at(hop(slab))})
             copy.start()
             started.append(copy)
         else:
@@ -449,8 +477,8 @@
     return [min(slots - 1, lead + (e * (slots - lead)) // count) for e in range(count)]
 
 
-def step_kernel(sizes, length, heads, head, slab_ref, x_ref, cot_ref, out_ref, y_ref, gx_ref,
-                buf, whi, wlo, xs, cots, fo_hi, fo_lo, so_hi, so_lo, cot_hi, cot_lo, gm_hi, gm_lo,
+def step_kernel(sizes, length, heads, head, mixer_ref, turned_ref, small_ref, up_ref, down_ref, x_ref, cot_ref, out_ref, y_ref, gx_ref,
+                slab_ref, buf, whi, wlo, xs, cots, fo_hi, fo_lo, so_hi, so_lo, cot_hi, cot_lo, gm_hi, gm_lo,
                 mixed, probs_hi, probs_lo, joined, mid, back, yb, staged, vec_ref, bias_ref, hidden_bias, small_grads,
                 swapped, landed, send_sem, recv_sem, swap_send, swap_recv,
                 push_send, push_recv, trade_send, trade_recv, stage_sem, image_sem, image_send, image_recv):
@@ -458,7 +486,7 @@
     number = functools.partial(slab_id, sizes=sizes)
     n = sizes[0] * sizes[1] * sizes[2]
     own, rows, width = xs.shape
-    share = slab_ref.shape[0]
+    share = up_ref.shape[0]
     hidden_local = hidden_bias.shape[-1]
     qkv, attn = 5 * LANES, 6 * LANES
     small, up = attn, attn + LANES
@@ -473,34 +501,36 @@
         return slice(*spans[p])
 
     def landing(p, slab, of):
-        return buf.at[of, block(slab, -1, of), span(p)]
-
-    def gather_event(p, slab):
-        spot = landing(p, slab, core)
+        return buf.at[core if of == "mine" else 1 - core, block(slab, -1, of), span(p)]
+
+    def gather_event(p, slab, along=(0, 1, 2), swap=True):
+        spot = landing(p, slab, "mine")
         if any(slab):
             pltpu.make_async_remote_copy(
                 src_ref=spot, dst_ref=spot, send_sem=send_sem.at[p, 0, 0], recv_sem=recv_sem.at[p, number(slab)],
                 device_id=partner).wait_recv()
         source = spot if any(slab) else slab_ref.at[:, span(p)]
-        for r in reversed(sends(slab, sizes)):
+        for r, steps, there in reversed(sends(slab, sizes)):
+            if r in along:
+                pltpu.make_async_remote_copy(
+                    src_ref=source, dst_ref=spot, send_sem=send_sem.at[p, r, number(there)],
+                    recv_sem=recv_sem.at[p, number(there)], device_id={"dp": at(steps)}).start()
+        if swap:
             pltpu.make_async_remote_copy(
-                src_ref=source, dst_ref=spot, send_sem=send_sem.at[p, r, number(slab)],
-                recv_sem=recv_sem.at[p, number(plus(slab, UNITS[r]))], device_id={"dp": at(UNITS[r])}).start()
-        pltpu.make_async_remote_copy(
-            src_ref=source, dst_ref=spot, send_sem=swap_send.at[p, number(slab)],
-            recv_sem=swap_recv.at[p, number(slab)], device_id=partner).start()
+                src_ref=source, dst_ref=spot, send_sem=swap_send.at[p, number(slab)],
+                recv_sem=swap_recv.at[p, number(slab)], device_id=partner).start()
 
     def gather_end(p):
         for slab in order:
-            spot = landing(p, slab, 1 - core)
+            spot = landing(p, slab, "other")
             pltpu.make_async_remote_copy(
                 src_ref=spot, dst_ref=spot, send_sem=swap_send.at[p, 0], recv_sem=swap_recv.at[p, number(slab)],
                 device_id=partner).wait_recv()
         for slab in order:
-            spot = landing(p, slab, core)
-            for r in sends(slab, sizes):
+            spot = landing(p, slab, "mine")
+            for r, _, there in sends(slab, sizes):
                 pltpu.make_async_remote_copy(
-                    src_ref=spot, dst_ref=spot, send_sem=send_sem.at[p, r, number(slab)],
+                    src_ref=spot, dst_ref=spot, send_sem=send_sem.at[p, r, number(there)],
                     recv_sem=recv_sem.at[p, 0], device_id=partner).wait_send()
             pltpu.make_async_remote_copy(
                 src_ref=spot, dst_ref=spot, send_sem=swap_send.at[p, number(slab)], recv_sem=swap_recv.at[p, 0],
@@ -515,7 +545,7 @@
     def trade(p, slab):
         s = number(slab)
         return pltpu.make_async_remote_copy(
-            src_ref=buf.at[1 - core, block(slab, 1, 1 - core), span(p)], dst_ref=swapped.at[s, :, span(p)],
+            src_ref=buf.at[1 - core, block(slab, 1, "other"), span(p)], dst_ref=swapped.at[s, :, span(p)],
             send_sem=trade_send.at[p, s], recv_sem=trade_recv.at[p, s], device_id=partner)
 
     def scatter_start(p):
@@ -530,19 +560,17 @@
 
     def push(p, slab):
         s = number(slab)
-        r = max(q for q in range(3) if slab[q])
         return pltpu.make_async_remote_copy(
-            src_ref=buf.at[core, block(slab, 1, core), span(p)], dst_ref=landed.at[s - 1, :, span(p)],
-            send_sem=push_send.at[p, s], recv_sem=push_recv.at[p, s], device_id={"dp": at(UNITS[r])})
+            src_ref=buf.at[core, block(slab, 1, "mine"), span(p)], dst_ref=landed.at[s - 1, :, span(p)],
+            send_sem=push_send.at[p, s], recv_sem=push_recv.at[p, s], device_id={"dp": at(hop(slab))})
 
     def scatter_event(p, slab):
         s = number(slab)
-        here = (core, block(slab, 1, core), span(p))
+        here = (core, block(slab, 1, "mine"), span(p))
         value = buf[here] + arrived(swapped, s, p, trade_recv.at[p, s])
-        for r in range(3):
-            if not any(slab[r + 1:]) and slab[r] + 1 < sizes[r]:
-                spot = number(plus(slab, UNITS[r]))
-                value = value + arrived(landed, spot - 1, p, push_recv.at[p, spot])
+        for other in sources(slab, sizes):
+            spot = number(other)
+            value = value + arrived(landed, spot - 1, p, push_recv.at[p, spot])
         if any(slab):
             buf[here] = value
             push(p, slab).start()
@@ -623,14 +651,21 @@
         place_in = (flat // piece) * head + owner * piece + flat % piece
         return (place_in == target + t * LANES).astype(f32).astype(bf16)
 
-    greet(core, at, -1)
+    pair = 2 * head
+    q, k, v = (mixer_ref[t] for t in range(3))
+    turned = turned_ref[...]
+    slab_ref[...] = jnp.concatenate(
+        [q[:, :pair], k[:, :pair], v[:, :pair], q[:, pair:], k[:, pair:], v[:, pair:], turned[:, pair:], turned[:, :pair],
+         small_ref[...], up_ref[...], down_ref[...]], axis=1)
+    greet(core, at, sizes)
     gather_event(0, (0, 0, 0))
+    gather_event(1, (0, 0, 0), (0,), False)
     staging = []
     tiles = width // LANES
     for t in range(tiles):
         staging.append(pltpu.make_async_copy(x_ref.at[:, t * LANES:(t + 1) * LANES], staged.at[t], stage_sem.at[t]))
         staging[-1].start()
-    buf[core, block((0, 0, 0), 1, core), :] = slab_ref[...]
+    buf[core, block((0, 0, 0), 1, "mine"), :] = slab_ref[...]
     xs[...] = jnp.zeros_like(xs)
     cots[...] = jnp.zeros_like(cots)
     small_grads[...] = jnp.zeros_like(small_grads)
@@ -646,7 +681,7 @@
 
     for slab in order[1:]:
         gather_event(0, slab)
-    gather_event(1, (0, 0, 0))
+    gather_event(1, (0, 0, 0), (1, 2))
     for i in range(own):
         cot_hi[i], cot_lo[i] = split(cots[i])
     gather_end(0)
@@ -681,12 +716,15 @@
             (side(w[3], 0) * score_scale, side(swap(w[3]), 0), side(w[4], 0)),
         ]
 
-    def serve(t, h, plan, event):
-        for slot, slab in plan:
-            if slot % heads == h:
-                pl.when(t == slot // heads)(functools.partial(event, 1, slab))
-
-    gather_plan = list(zip(spread(len(order) - 1, 2 * own * heads, 1), order[1:]))
+    def serve(t, plan, event):
+        for slot in sorted({slot for slot, _ in plan}):
+            @pl.when(t == slot)
+            def _(slot=slot):
+                for when, slab in plan:
+                    if when == slot:
+                        event(1, slab)
+
+    gather_plan = list(zip(spread(len(order) - 1, 2 * own, 0), order[1:]))
 
     def attend(t, _):
         i, c = t // 2, t % 2
@@ -697,10 +735,10 @@
             fo_hi[i], fo_lo[i] = split(normed * vec(0) + vec(1))
             mid[i] = xs[i] + vec(2)
 
+        serve(t, gather_plan, gather_event)
         mixed[i, c] = product((fo_hi[i], fo_lo[i]), weight(c, 0, qkv), 1, 0) + bias_ref[c]
         outs = []
         for h, (q, k, v) in enumerate(windows(i, c)):
-            serve(t, h, gather_plan, gather_event)
             scores = product(split(q), split(k), 1, 1)
             scores = jnp.where(column < length, scores, MASKED)
             expon = jnp.exp(scores - jnp.max(scores, axis=-1, keepdims=True))
@@ -752,20 +790,20 @@
             gm_hi[i], gm_lo[i] = split(grad_middle)
             back[i] = grad_middle
             mid[i] = jnp.zeros((rows, width), f32)
+            keep, give, _ = image_copies(0, yb, y_ref, i)
+            keep.start()
+            give.start()
 
         return 0
 
     lax.fori_loop(0, 2 * own, feed, 0)
 
     scatter_start(1)
-    for i in range(own):
-        keep, give, _ = image_copies(0, yb, y_ref, i)
-        keep.start()
-        give.start()
-    scatter_plan = list(zip(spread(len(back_order), 2 * own * heads, 1), back_order))
+    scatter_plan = list(zip(spread(len(back_order) - 1, 2 * own, 1), back_order[:-1]))
 
     def attend_back(t, _):
         i, c = t // 2, t % 2
+        serve(t, scatter_plan, scatter_event)
         gm = (gm_hi[i], gm_lo[i])
         fo = (fo_hi[i], fo_lo[i])
         grad_heads = product(gm, weight(c, 4 * LANES, attn), 1, 0)
@@ -776,16 +814,15 @@
         outs = (pair_out, pair_out, single_out)
         grads = []
         for h, (q, k, v) in enumerate(windows(i, c)):
-            serve(t, h, scatter_plan, scatter_event)
             grad_out = grad_outs[h]
             row = jnp.sum(grad_out * outs[h], axis=-1, keepdims=True)
             grad_out = split(grad_out)
             grad_probs = product(grad_out, split(v), 1, 1)
             probs = (probs_hi[i, c, h], probs_lo[i, c, h])
-            grad_v = product(probs, grad_out, 0, 0)
+            grad_v = product_apart(probs, grad_out, 0, 0)
             grad_scores = split((probs[0].astype(f32) + probs[1].astype(f32)) * (grad_probs - row))
             grad_q = product_apart(grad_scores, split(k), 1, 0) * score_scale
-            grad_k = product(grad_scores, split(q), 0, 0)
+            grad_k = product_apart(grad_scores, split(q), 0, 0)
             grads.append((grad_q, grad_k, grad_v))
         one, two, three = grads
         grad_mixed = jnp.concatenate(
@@ -802,6 +839,9 @@
             small_grads[0, 0:1, 0:width] += total(grad_first * first)
             small_grads[0, 1:2, 0:width] += total(grad_first)
             xs[i] = back[i] + norm_back(grad_first, first, first_inverse, vec(0))
+            keep, give, _ = image_copies(1, xs, gx_ref, i)
+            keep.start()
+            give.start()
 
         return 0
 
@@ -815,11 +855,9 @@
         packed = jnp.concatenate([six, bias, hidden[0], hidden[1], jnp.zeros((LANES - 9, width), f32)], axis=0)
         buf[c, :, small:up] = packed.T
     scatter_start(0)
-    for i in range(own):
-        keep, give, _ = image_copies(1, xs, gx_ref, i)
-        keep.start()
-        give.start()
     for slab in back_order:
+        if slab == back_order[-first_size]:
+            scatter_event(1, back_order[-1])
         scatter_event(0, slab)
     for t, source, ref in ((0, yb, y_ref), (1, xs, gx_ref)):
         for i in range(own):
@@ -831,14 +869,14 @@
     scatter_end(0)
 
 
-def run_step(slab, inputs, cotangent, n, heads, head, length):
+def run_step(mixer, turned, small, up, down, inputs, cotangent, n, heads, head, length):
     sizes = rings(n)
     width = inputs.shape[1]
     images = inputs.shape[0] // length
     own = images // 2
     rows = -(-length // 16) * 16
-    share, columns = slab.shape
-    hidden_local = (columns - 7 * LANES) // 2
+    share, hidden_local = up.shape
+    columns = 7 * LANES + 2 * hidden_local
     anywhere = pl.BlockSpec(memory_space=pl.ANY)
     act = pltpu.VMEM((own, rows, width), bf16)
     full = pltpu.VMEM((own, rows, width), f32)
@@ -846,11 +884,12 @@
     probs = pltpu.VMEM((own, 2, heads, rows, rows), bf16)
     return pl.pallas_call(
         functools.partial(step_kernel, sizes, length, heads, head),
-        out_shape=[jax.ShapeDtypeStruct(slab.shape, f32), jax.ShapeDtypeStruct((images, rows, width), f32),
+        out_shape=[jax.ShapeDtypeStruct((share, columns), f32), jax.ShapeDtypeStruct((images, rows, width), f32),
                    jax.ShapeDtypeStruct((images, rows, width), f32)],
-        in_specs=[pl.BlockSpec(memory_space=pltpu.VMEM), anywhere, anywhere],
+        in_specs=[pl.BlockSpec(memory_space=pltpu.VMEM)] * 5 + [anywhere] * 2,
         out_specs=[pl.BlockSpec(memory_space=pltpu.VMEM), anywhere, anywhere],
         scratch_shapes=[
+            pltpu.VMEM((share, columns), f32),
             pltpu.VMEM((2, width, columns), f32),
             pltpu.VMEM((2, width, columns), bf16), pltpu.VMEM((2, width, columns), bf16),
             full, full, act, act, act, act, act, act, act, act,
@@ -867,7 +906,7 @@
         compiler_params=pltpu.CompilerParams(
             collective_id=2, has_side_effects=True, vmem_limit_bytes=67043328),
         name="step",
-    )(slab, inputs, cotangent)
+    )(mixer, turned, small, up, down, inputs, cotangent)
 
 
 def pack_attention(mixer, output):
@@ -944,14 +983,12 @@
     head = piece * n
     hidden_local = params["expand_weight"].shape[1]
     small = jnp.pad(pack_small(params).reshape(-1, share).T, ((0, 0), (0, LANES - 9)))
-    slab = jnp.concatenate([
-        pack_attention(params["mixer_weight"], params["output_weight"]), small,
-        params["expand_weight"], params["reduce_weight"].T], axis=1)
-
     def tokens(v):
         return v.transpose(1, 0, 2).reshape(length * images, width)
 
-    summed, block_out, input_gradient = run_step(slab, tokens(inputs), tokens(cotangent), n, heads, head, length)
+    summed, block_out, input_gradient = run_step(
+        params["mixer_weight"].transpose(1, 0, 2), params["output_weight"].T, small, params["expand_weight"],
+        params["reduce_weight"].T, tokens(inputs), tokens(cotangent), n, heads, head, length)
     summed = summed * scale
     mixer, output = unpack_attention(summed[:, :6 * LANES], head)
     gradients = unpack_small(summed[:, 6 * LANES:6 * LANES + 9].T.reshape(-1), params)

time: 187 us -> 162 us (0.87)
  Pallas kernels: 164 us -> 142 us
  local copies, waits for them, and re-layouts: 16.3 us -> 13 us
    pallas_call x1, Pallas kernels: 164 us -> 142 us  [run_step(): pl.pallas_call(functools.partial(step_kernel, sizes, length, heads, head)...]
where the time goes in v3:
time: 162 us; the launch traced here: 161 us
  Pallas kernels  142 us (88%)
  local copies, waits for them, and re-layouts  13 us (8%)
  other arithmetic  5.19 us (3%)
    pallas_call x1, Pallas kernels, run_step(): pl.pallas_call(functools.partial(step_kernel, sizes, length, heads, head)...  142 us
    unnamed x99, local copies, waits for them, and re-layouts  8.49 us
    sub x9, other arithmetic, adam_update(): param - learn_rate * (mean_hat / (jnp.sqrt(square_hat) + adam_eps) + deca...  5.15 us

profile of v3, /device:TPU:0, one launch (start us, length us, event | category | flops | bytes accessed | tf_op | source)
XLA Modules:
  0.0 161.4 jit_solution(10271590378827524782)
XLA Ops:
  0.7 0.7 copy.131
  1.4 0.1 reshape.132
  1.5 0.8 copy.132
  2.3 0.1 reshape.133
  2.3 0.8 concatenate.19
  3.2 0.1 reshape.134
  3.2 0.1 copy.133
  3.3 0.6 pad.4.small_ref
  3.9 141.8 %step.1 = (f32[24,2432]{1,0:T(8,128)}, f32[8,208,384]{2,1,0:T(8,128)}, f32[8,208,384]{2,1,0:T(8,128)}) custom-call(f32[3,24,192]{2,1,0:T(8,128)} %bitcast.26, f32[24,192]{1,0:T(8,128)} %bitcast.28, f32[24,128]{1,0:T(8,128)} %pad.4.small_ref, f32[24,768]{1,0:T(8,128)} %up_ref.1, f32[24,768]{1,0:T(8,128)} %bitcast.27, f32[1576,384]{1,0:T(8,128)} %bitcast.24, ...), custom_call_target="tpu_custom_call" | custom-call | tf_op jit(solution)/shard_map/step/pallas_call | solution.py:885
  145.7 1.9 %slice.104 = f32[8,197,384]{2,1,0:T(8,128)S(1)} slice(f32[8,208,384]{2,1,0:T(8,128)} %get-tuple-element.53), slice={[0:8], [0:197], [0:384]} | slice | bytes 4841472 | tf_op jit(solution)/shard_map/slice | solution.py:998
  147.6 1.9 %copy.142 = f32[8,197,384]{2,0,1:T(8,128)} copy(f32[8,197,384]{2,1,0:T(8,128)S(1)} %slice.104) | data formatting | bytes 4841472
  149.5 0.6 copy-done
  150.1 0.2 slice.105
  150.2 0.0 copy-start.1
  150.3 0.0 copy-start.6
  150.3 0.0 copy-start.7
  150.3 0.0 copy-start.5
  150.3 0.0 copy-start.12
  150.3 0.0 copy-start.13
  150.3 0.0 copy-start.2
  150.3 0.0 copy-start.8
  150.3 0.0 copy-start.9
  150.4 0.0 copy-start.3
  150.4 0.0 copy-start.10
  150.4 0.0 copy-start.11
  150.4 1.9 %copy.143 = f32[8,197,384]{2,0,1:T(8,128)} copy(f32[8,197,384]{2,1,0:T(8,128)S(1)} %slice.105) | data formatting | bytes 4841472
  152.3 0.0 copy-start.35
  152.3 0.0 copy-start.36
  152.3 0.0 copy-start.14
  152.3 0.0 copy-start.17
  152.3 0.0 copy-start.18
  152.4 0.0 copy-start.37
  152.4 0.0 copy-start.38
  152.4 0.0 copy-start.29
  152.4 0.0 copy-start.30
  152.4 0.0 copy-start.42
  152.4 0.0 copy-start.43
  152.5 0.0 copy-start.31
  152.5 0.0 copy-start.32
  152.6 0.3 slice_reduce_fusion
  152.9 0.0 copy-start.20
  152.9 0.0 copy-start.21
  152.9 0.0 copy-start.22
  152.9 0.0 copy-start.23
  152.9 0.0 copy-start.24
  152.9 0.1 fusion.27
  153.1 0.8 multiply_subtract_fusion.2
  153.8 0.1 reshape.137
  153.9 0.6 copy.144
  154.5 0.6 multiply_subtract_fusion.3
  155.2 0.7 multiply_subtract_fusion.1
  155.9 0.1 slice.147
  156.0 0.1 copy.134
  156.0 0.1 reshape.138
  156.1 0.1 copy.145
  156.2 0.0 copy-start.16
  156.2 0.8 multiply_subtract_fusion
  157.0 0.5 multiply_subtract_fusion.10
  157.6 0.6 copy.146
  158.2 0.5 multiply_subtract_fusion.8
  158.8 0.5 multiply_subtract_fusion.6
  159.4 0.6 multiply_subtract_fusion.5
  160.0 0.6 copy.147
  160.6 0.6 copy.148
  (64 shorter events, 0.2 us)
Async XLA Ops:
  147.6 2.5 %copy-start = (f32[8,208,384]{2,1,0:T(8,128)S(1)}, f32[8,208,384]{2,1,0:T(8,128)}, u32[]{:S(2)}) copy-start(f32[8,208,384]{2,1,0:T(8,128)} %get-tuple-element.54) | copy-start | bytes 7667716
  150.2 2.3 %copy-start.4 = (f32[24,2432]{1,0:T(8,128)S(1)}, f32[24,2432]{1,0:T(8,128)}, u32[]{:S(2)}) copy-start(f32[24,2432]{1,0:T(8,128)} %get-tuple-element.55) | copy-start | bytes 700420
  150.2 2.8 %copy-start.1 = (f32[24,3,192]{2,0,1:T(8,128)S(1)}, f32[24,3,192]{2,0,1:T(8,128)}, u32[]{:S(2)}) copy-start(f32[24,3,192]{2,0,1:T(8,128)} %param.42) | copy-start | bytes 165892
  150.3 2.8 %copy-start.6 = (f32[24,3,192]{2,0,1:T(8,128)S(1)}, f32[24,3,192]{2,0,1:T(8,128)}, u32[]{:S(2)}) copy-start(f32[24,3,192]{2,0,1:T(8,128)} %param.54) | copy-start | bytes 165892
  150.3 2.8 %copy-start.7 = (f32[24,3,192]{2,0,1:T(8,128)S(1)}, f32[24,3,192]{2,0,1:T(8,128)}, u32[]{:S(2)}) copy-start(f32[24,3,192]{2,0,1:T(8,128)} %param.66) | copy-start | bytes 165892
  150.3 4.2 %copy-start.5 = (f32[192,24]{0,1:T(8,128)S(1)}, f32[192,24]{0,1:T(8,128)}, u32[]{:S(2)}) copy-start(f32[192,24]{0,1:T(8,128)} %param.44) | copy-start | bytes 55300
  150.3 4.2 %copy-start.12 = (f32[192,24]{0,1:T(8,128)S(1)}, f32[192,24]{0,1:T(8,128)}, u32[]{:S(2)}) copy-start(f32[192,24]{0,1:T(8,128)} %param.56) | copy-start | bytes 55300
  150.3 4.2 %copy-start.13 = (f32[192,24]{0,1:T(8,128)S(1)}, f32[192,24]{0,1:T(8,128)}, u32[]{:S(2)}) copy-start(f32[192,24]{0,1:T(8,128)} %param.68) | copy-start | bytes 55300
  150.3 4.8 %copy-start.2 = (f32[24,768]{1,0:T(8,128)S(1)}, f32[24,768]{1,0:T(8,128)}, u32[]{:S(2)}) copy-start(f32[24,768]{1,0:T(8,128)} %up_ref.1) | copy-start | bytes 221188
  150.3 4.8 %copy-start.8 = (f32[24,768]{1,0:T(8,128)S(1)}, f32[24,768]{1,0:T(8,128)}, u32[]{:S(2)}) copy-start(f32[24,768]{1,0:T(8,128)} %param.60) | copy-start | bytes 221188
  150.3 4.8 %copy-start.9 = (f32[24,768]{1,0:T(8,128)S(1)}, f32[24,768]{1,0:T(8,128)}, u32[]{:S(2)}) copy-start(f32[24,768]{1,0:T(8,128)} %param.72) | copy-start | bytes 221188
  150.4 5.9 %copy-start.3 = (f32[768,24]{0,1:T(8,128)S(1)}, f32[768,24]{0,1:T(8,128)}, u32[]{:S(2)}) copy-start(f32[768,24]{0,1:T(8,128)} %param.50) | copy-start | bytes 221188
  150.4 5.9 %copy-start.10 = (f32[768,24]{0,1:T(8,128)S(1)}, f32[768,24]{0,1:T(8,128)}, u32[]{:S(2)}) copy-start(f32[768,24]{0,1:T(8,128)} %param.62) | copy-start | bytes 221188
  150.4 5.8 %copy-start.11 = (f32[768,24]{0,1:T(8,128)S(1)}, f32[768,24]{0,1:T(8,128)}, u32[]{:S(2)}) copy-start(f32[768,24]{0,1:T(8,128)} %param.74) | copy-start | bytes 221188
  152.3 4.7 %copy-start.25 = (f32[24]{0:T(128)S(1)}, f32[24]{0:T(128)}, u32[]{:S(2)}) copy-start(f32[24]{0:T(128)} %param.40) | copy-start | bytes 292
  152.3 4.7 %copy-start.26 = (f32[24]{0:T(128)S(1)}, f32[24]{0:T(128)}, u32[]{:S(2)}) copy-start(f32[24]{0:T(128)} %param.41) | copy-start | bytes 292
  152.3 4.7 %copy-start.33 = (f32[24]{0:T(128)S(1)}, f32[24]{0:T(128)}, u32[]{:S(2)}) copy-start(f32[24]{0:T(128)} %param.53) | copy-start | bytes 292
  152.3 4.8 %copy-start.34 = (f32[24]{0:T(128)S(1)}, f32[24]{0:T(128)}, u32[]{:S(2)}) copy-start(f32[24]{0:T(128)} %param.65) | copy-start | bytes 292
  152.3 4.8 %copy-start.35 = (f32[24]{0:T(128)S(1)}, f32[24]{0:T(128)}, u32[]{:S(2)}) copy-start(f32[24]{0:T(128)} %param.64) | copy-start | bytes 292
  152.3 4.8 %copy-start.36 = (f32[24]{0:T(128)S(1)}, f32[24]{0:T(128)}, u32[]{:S(2)}) copy-start(f32[24]{0:T(128)} %param.52) | copy-start | bytes 292
  152.3 5.3 %copy-start.14 = (f32[2,3,4]{2,0,1:T(2,128)S(1)}, f32[2,3,4]{2,0,1:T(2,128)}, u32[]{:S(2)}) copy-start(f32[2,3,4]{2,0,1:T(2,128)} %param.43) | copy-start | bytes 292
  152.3 5.3 %copy-start.17 = (f32[2,3,4]{2,0,1:T(2,128)S(1)}, f32[2,3,4]{2,0,1:T(2,128)}, u32[]{:S(2)}) copy-start(f32[2,3,4]{2,0,1:T(2,128)} %param.55) | copy-start | bytes 292
  152.3 5.3 %copy-start.18 = (f32[2,3,4]{2,0,1:T(2,128)S(1)}, f32[2,3,4]{2,0,1:T(2,128)}, u32[]{:S(2)}) copy-start(f32[2,3,4]{2,0,1:T(2,128)} %param.67) | copy-start | bytes 292
  152.3 5.9 %copy-start.27 = (f32[24]{0:T(128)S(1)}, f32[24]{0:T(128)}, u32[]{:S(2)}) copy-start(f32[24]{0:T(128)} %param.45) | copy-start | bytes 292
  152.3 5.9 %copy-start.28 = (f32[24]{0:T(128)S(1)}, f32[24]{0:T(128)}, u32[]{:S(2)}) copy-start(f32[24]{0:T(128)} %param.46) | copy-start | bytes 292
  152.4 5.9 %copy-start.37 = (f32[24]{0:T(128)S(1)}, f32[24]{0:T(128)}, u32[]{:S(2)}) copy-start(f32[24]{0:T(128)} %param.58) | copy-start | bytes 292
  152.4 5.9 %copy-start.38 = (f32[24]{0:T(128)S(1)}, f32[24]{0:T(128)}, u32[]{:S(2)}) copy-start(f32[24]{0:T(128)} %param.70) | copy-start | bytes 292
  152.4 5.9 %copy-start.39 = (f32[24]{0:T(128)S(1)}, f32[24]{0:T(128)}, u32[]{:S(2)}) copy-start(f32[24]{0:T(128)} %param.69) | copy-start | bytes 292
  152.4 5.9 %copy-start.40 = (f32[24]{0:T(128)S(1)}, f32[24]{0:T(128)}, u32[]{:S(2)}) copy-start(f32[24]{0:T(128)} %param.57) | copy-start | bytes 292
  152.4 6.4 %copy-start.29 = (f32[24]{0:T(128)S(1)}, f32[24]{0:T(128)}, u32[]{:S(2)}) copy-start(f32[24]{0:T(128)} %param.47) | copy-start | bytes 292
  152.4 6.4 %copy-start.30 = (f32[24]{0:T(128)S(1)}, f32[24]{0:T(128)}, u32[]{:S(2)}) copy-start(f32[24]{0:T(128)} %param.51) | copy-start | bytes 292
  152.4 6.4 %copy-start.41 = (f32[24]{0:T(128)S(1)}, f32[24]{0:T(128)}, u32[]{:S(2)}) copy-start(f32[24]{0:T(128)} %param.63) | copy-start | bytes 292
  152.4 6.4 %copy-start.42 = (f32[24]{0:T(128)S(1)}, f32[24]{0:T(128)}, u32[]{:S(2)}) copy-start(f32[24]{0:T(128)} %param.75) | copy-start | bytes 292
  152.4 6.4 %copy-start.43 = (f32[24]{0:T(128)S(1)}, f32[24]{0:T(128)}, u32[]{:S(2)}) copy-start(f32[24]{0:T(128)} %param.71) | copy-start | bytes 292
  152.5 6.4 %copy-start.44 = (f32[24]{0:T(128)S(1)}, f32[24]{0:T(128)}, u32[]{:S(2)}) copy-start(f32[24]{0:T(128)} %param.59) | copy-start | bytes 292
  152.5 6.9 %copy-start.15 = (f32[12,4]{0,1:T(4,128)S(1)}, f32[12,4]{0,1:T(4,128)}, u32[]{:S(2)}) copy-start(f32[12,4]{0,1:T(4,128)} %param.49) | copy-start | bytes 580
  152.5 6.9 %copy-start.31 = (f32[12,4]{0,1:T(4,128)S(1)}, f32[12,4]{0,1:T(4,128)}, u32[]{:S(2)}) copy-start(f32[12,4]{0,1:T(4,128)} %param.61) | copy-start | bytes 580
  152.5 6.9 %copy-start.32 = (f32[12,4]{0,1:T(4,128)S(1)}, f32[12,4]{0,1:T(4,128)}, u32[]{:S(2)}) copy-start(f32[12,4]{0,1:T(4,128)} %param.73) | copy-start | bytes 580
  152.9 8.3 %copy-start.19 = (f32[24]{0:T(128)}, f32[24]{0:T(128)S(1)}, u32[]{:S(2)}) copy-start(f32[24]{0:T(128)S(1)} %get-tuple-element.206) | copy-start | bytes 292
  152.9 8.3 %copy-start.20 = (f32[24]{0:T(128)}, f32[24]{0:T(128)S(1)}, u32[]{:S(2)}) copy-start(f32[24]{0:T(128)S(1)} %get-tuple-element.207) | copy-start | bytes 292
  152.9 8.3 %copy-start.21 = (f32[24]{0:T(128)}, f32[24]{0:T(128)S(1)}, u32[]{:S(2)}) copy-start(f32[24]{0:T(128)S(1)} %get-tuple-element.208) | copy-start | bytes 292
  152.9 8.3 %copy-start.22 = (f32[24]{0:T(128)}, f32[24]{0:T(128)S(1)}, u32[]{:S(2)}) copy-start(f32[24]{0:T(128)S(1)} %get-tuple-element.209) | copy-start | bytes 292
  152.9 8.3 %copy-start.23 = (f32[24]{0:T(128)}, f32[24]{0:T(128)S(1)}, u32[]{:S(2)}) copy-start(f32[24]{0:T(128)S(1)} %get-tuple-element.211) | copy-start | bytes 292
  152.9 8.3 %copy-start.24 = (f32[24]{0:T(128)}, f32[24]{0:T(128)S(1)}, u32[]{:S(2)}) copy-start(f32[24]{0:T(128)S(1)} %get-tuple-element.212) | copy-start | bytes 292
  156.2 5.0 %copy-start.16 = (f32[12,4]{0,1:T(4,128)}, f32[12,4]{0,1:T(4,128)S(1)}, u32[]{:S(2)}) copy-start(f32[12,4]{0,1:T(4,128)S(1)} %copy.145) | copy-start | bytes 580

commit v4 on v3

--- a/solution.py
+++ b/solution.py
@@ -479,7 +479,7 @@
 
 def step_kernel(sizes, length, heads, head, mixer_ref, turned_ref, small_ref, up_ref, down_ref, x_ref, cot_ref, out_ref, y_ref, gx_ref,
                 slab_ref, buf, whi, wlo, xs, cots, fo_hi, fo_lo, so_hi, so_lo, cot_hi, cot_lo, gm_hi, gm_lo,
-                mixed, probs_hi, probs_lo, joined, mid, back, yb, staged, vec_ref, bias_ref, hidden_bias, small_grads,
+                mixed, probs_hi, probs_lo, joined, mid, back, yb, staged, vec_ref, bias_ref, hidden_bias, small_grads, mixed_hot, hidden_hot,
                 swapped, landed, send_sem, recv_sem, swap_send, swap_recv,
                 push_send, push_recv, trade_send, trade_recv, stage_sem, image_sem, image_send, image_recv):
     core, at = place(sizes)
@@ -633,23 +633,26 @@
         return high, middle_term, (v - middle_term.astype(f32)).astype(bf16)
 
     def moved(v, onehot, dim):
-        return sum(dot(term, onehot, 1, dim) for term in reversed(thirds(v)))
+        terms = jnp.concatenate([term.astype(f32) for term in thirds(v)], axis=0).astype(bf16)
+        out = dot(terms, onehot, 1, dim)
+        return out[4:6] + out[2:4] + out[0:2]
 
     piece = head // n
-    entry = lax.broadcasted_iota(jnp.int32, (width, LANES), 0)
-    owner, inner = entry // share, entry % share
-    target = lax.broadcasted_iota(jnp.int32, (width, LANES), 1)
-
-    def attention_bias_at(t):
+
+    def make_onehots():
+        entry = lax.broadcasted_iota(jnp.int32, (width, LANES), 0)
+        owner, inner = entry // share, entry % share
+        target = lax.broadcasted_iota(jnp.int32, (width, LANES), 1)
         kind, which = inner // (heads * piece), (inner // piece) % heads
         window = jnp.where(kind == 0, jnp.where(which < 2, 0, 3), jnp.where(which < 2, 2, 4))
-        place_in = (which % 2) * head + owner * piece + inner % piece
-        return ((window == t) & (place_in == target)).astype(f32).astype(bf16)
-
-    def hidden_bias_at(half, t):
-        flat = inner + half * share
-        place_in = (flat // piece) * head + owner * piece + flat % piece
-        return (place_in == target + t * LANES).astype(f32).astype(bf16)
+        spot = window * LANES + (which % 2) * head + owner * piece + inner % piece
+        for t in range(5):
+            mixed_hot[:, t * LANES:(t + 1) * LANES] = (spot == target + t * LANES).astype(f32).astype(bf16)
+        for half in range(2):
+            flat = inner + half * share
+            spot = (flat // piece) * head + owner * piece + flat % piece
+            for t in range(hidden_local // LANES):
+                hidden_hot[half, :, t * LANES:(t + 1) * LANES] = (spot == target + t * LANES).astype(f32).astype(bf16)
 
     pair = 2 * head
     q, k, v = (mixer_ref[t] for t in range(3))
@@ -659,7 +662,7 @@
          small_ref[...], up_ref[...], down_ref[...]], axis=1)
     greet(core, at, sizes)
     gather_event(0, (0, 0, 0))
-    gather_event(1, (0, 0, 0), (0,), False)
+    gather_event(1, (0, 0, 0), (0, 1, 2))
     staging = []
     tiles = width // LANES
     for t in range(tiles):
@@ -679,22 +682,23 @@
             for i in range(own):
                 sink[i, 0:length, lanes] = staged[t, pl.ds(core * own + i, length, stride=2 * own), :]
 
+    make_onehots()
     for slab in order[1:]:
         gather_event(0, slab)
-    gather_event(1, (0, 0, 0), (1, 2))
     for i in range(own):
         cot_hi[i], cot_lo[i] = split(cots[i])
     gather_end(0)
+    turned = [buf[c, :, small:up].T[0:16] for c in range(2)]
+    vec_ref[...] = turned[0][0:8, :]
+
+    def both(r):
+        return jnp.concatenate([turned[0][r:r + 1], turned[1][r:r + 1]], axis=0)
+
+    bias = moved(both(6), mixed_hot[...], 0)
+    hidden = moved(both(7), hidden_hot[0], 0) + moved(both(8), hidden_hot[1], 0)
     for c in range(2):
-        turned = buf[c, :, small:up].T
-        if c == 0:
-            vec_ref[...] = turned[0:8, :]
-        packed = turned[0:16, :]
-        for t in range(5):
-            bias_ref[c, :, t * LANES:(t + 1) * LANES] = moved(packed[6:7], attention_bias_at(t), 0)
-        for t in range(hidden_local // LANES):
-            hidden_bias[c, :, t * LANES:(t + 1) * LANES] = (
-                moved(packed[7:8], hidden_bias_at(0, t), 0) + moved(packed[8:9], hidden_bias_at(1, t), 0))
+        bias_ref[c] = bias[c:c + 1]
+        hidden_bias[c] = hidden[c:c + 1]
     convert(0, attn)
 
     lane = lax.broadcasted_iota(jnp.int32, (rows, LANES), 1)
@@ -847,12 +851,13 @@
 
     lax.fori_loop(0, 2 * own, attend_back, 0)
 
+    bias = moved(jnp.concatenate([small_grads[c, 6:7, 0:qkv] for c in range(2)], axis=0), mixed_hot[...], 1)
+    hidden = [moved(jnp.concatenate([small_grads[c, 7:8, :] for c in range(2)], axis=0), hidden_hot[half], 1)
+              for half in range(2)]
+    six = small_grads[0, 0:6, 0:width]
     for c in range(2):
-        bias = sum(moved(small_grads[c, 6:7, t * LANES:(t + 1) * LANES], attention_bias_at(t), 1) for t in range(5))
-        hidden = [sum(moved(small_grads[c, 7:8, t * LANES:(t + 1) * LANES], hidden_bias_at(half, t), 1)
-                      for t in range(hidden_local // LANES)) for half in range(2)]
-        six = small_grads[0, 0:6, 0:width]
-        packed = jnp.concatenate([six, bias, hidden[0], hidden[1], jnp.zeros((LANES - 9, width), f32)], axis=0)
+        packed = jnp.concatenate([six, bias[c:c + 1], hidden[0][c:c + 1], hidden[1][c:c + 1],
+                                  jnp.zeros((LANES - 9, width), f32)], axis=0)
         buf[c, :, small:up] = packed.T
     scatter_start(0)
     for slab in back_order:
@@ -898,6 +903,7 @@
             pltpu.VMEM((width // LANES, inputs.shape[0], LANES), f32),
             pltpu.VMEM((8, width), f32), pltpu.VMEM((2, 1, 5 * LANES), f32), pltpu.VMEM((2, 1, hidden_local), f32),
             pltpu.VMEM((2, 8, hidden_local), f32),
+            pltpu.VMEM((width, 5 * LANES), bf16), pltpu.VMEM((2, width, hidden_local), bf16),
             pltpu.VMEM((n, share, columns), f32), pltpu.VMEM((n - 1, share, columns), f32),
             dma((2, 3, n)), dma((2, n)), dma((2, n)), dma((2, n)),
             dma((2, n)), dma((2, n)), dma((2, n)), dma((2, n)),

time: 162 us -> 156 us (0.963)
  Pallas kernels: 142 us -> 136 us
    pallas_call x1, Pallas kernels: 142 us -> 136 us  [run_step(): pl.pallas_call(functools.partial(step_kernel, sizes, length, heads, head)...]
where the time goes in v4:
time: 156 us; the launch traced here: 155 us
  Pallas kernels  136 us (87%)
  local copies, waits for them, and re-layouts  13 us (8%)
  other arithmetic  5.19 us (3%)
    pallas_call x1, Pallas kernels, run_step(): pl.pallas_call(functools.partial(step_kernel, sizes, length, heads, head)...  136 us
    unnamed x99, local copies, waits for them, and re-layouts  8.49 us
    sub x9, other arithmetic, adam_update(): param - learn_rate * (mean_hat / (jnp.sqrt(square_hat) + adam_eps) + deca...  5.15 us

profile of v4, /device:TPU:0, one launch (start us, length us, event | category | flops | bytes accessed | tf_op | source)
XLA Modules:
  0.0 155.2 jit_solution(12235348309446777300)
XLA Ops:
  0.7 0.7 copy.131
  1.4 0.1 reshape.132
  1.5 0.8 copy.132
  2.3 0.1 reshape.133
  2.3 0.8 concatenate.19
  3.2 0.1 reshape.134
  3.2 0.1 copy.133
  3.3 0.6 pad.4.small_ref
  3.9 135.7 %step.1 = (f32[24,2432]{1,0:T(8,128)}, f32[8,208,384]{2,1,0:T(8,128)}, f32[8,208,384]{2,1,0:T(8,128)}) custom-call(f32[3,24,192]{2,1,0:T(8,128)} %bitcast.26, f32[24,192]{1,0:T(8,128)} %bitcast.28, f32[24,128]{1,0:T(8,128)} %pad.4.small_ref, f32[24,768]{1,0:T(8,128)} %up_ref.1, f32[24,768]{1,0:T(8,128)} %bitcast.27, f32[1576,384]{1,0:T(8,128)} %bitcast.24, ...), custom_call_target="tpu_custom_call" | custom-call | tf_op jit(solution)/shard_map/step/pallas_call | solution.py:890
  139.6 1.9 %slice.104 = f32[8,197,384]{2,1,0:T(8,128)S(1)} slice(f32[8,208,384]{2,1,0:T(8,128)} %get-tuple-element.53), slice={[0:8], [0:197], [0:384]} | slice | bytes 4841472 | tf_op jit(solution)/shard_map/slice | solution.py:1004
  141.5 1.9 %copy.142 = f32[8,197,384]{2,0,1:T(8,128)} copy(f32[8,197,384]{2,1,0:T(8,128)S(1)} %slice.104) | data formatting | bytes 4841472
  143.3 0.6 copy-done
  143.9 0.2 slice.105
  144.1 0.0 copy-start.1
  144.1 0.0 copy-start.6
  144.1 0.0 copy-start.7
  144.2 0.0 copy-start.5
  144.2 0.0 copy-start.12
  144.2 0.0 copy-start.13
  144.2 0.0 copy-start.2
  144.2 0.0 copy-start.8
  144.2 0.0 copy-start.9
  144.2 0.0 copy-start.3
  144.2 0.0 copy-start.10
  144.3 0.0 copy-start.11
  144.3 1.9 %copy.143 = f32[8,197,384]{2,0,1:T(8,128)} copy(f32[8,197,384]{2,1,0:T(8,128)S(1)} %slice.105) | data formatting | bytes 4841472
  146.1 0.0 copy-start.35
  146.1 0.0 copy-start.36
  146.2 0.0 copy-start.14
  146.2 0.0 copy-start.17
  146.2 0.0 copy-start.18
  146.2 0.0 copy-start.27
  146.2 0.0 copy-start.38
  146.2 0.0 copy-start.39
  146.3 0.0 copy-start.30
  146.3 0.0 copy-start.41
  146.3 0.0 copy-start.44
  146.3 0.0 copy-start.15
  146.4 0.0 copy-start.32
  146.4 0.3 slice_reduce_fusion
  146.7 0.0 copy-start.20
  146.8 0.0 copy-start.21
  146.8 0.0 copy-start.22
  146.8 0.0 copy-start.23
  146.8 0.0 copy-start.24
  146.8 0.1 fusion.27
  146.9 0.8 multiply_subtract_fusion.2
  147.7 0.1 reshape.137
  147.8 0.6 copy.144
  148.4 0.6 multiply_subtract_fusion.3
  149.0 0.7 multiply_subtract_fusion.1
  149.8 0.1 slice.147
  149.8 0.1 copy.134
  149.9 0.1 reshape.138
  150.0 0.1 copy.145
  150.1 0.0 copy-start.16
  150.1 0.8 multiply_subtract_fusion
  150.9 0.5 multiply_subtract_fusion.10
  151.5 0.6 copy.146
  152.1 0.5 multiply_subtract_fusion.8
  152.7 0.5 multiply_subtract_fusion.6
  153.3 0.6 multiply_subtract_fusion.5
  153.9 0.6 copy.147
  154.5 0.6 copy.148
  (64 shorter events, 0.2 us)
Async XLA Ops:
  141.5 2.5 %copy-start = (f32[8,208,384]{2,1,0:T(8,128)S(1)}, f32[8,208,384]{2,1,0:T(8,128)}, u32[]{:S(2)}) copy-start(f32[8,208,384]{2,1,0:T(8,128)} %get-tuple-element.54) | copy-start | bytes 7667716
  144.1 2.3 %copy-start.4 = (f32[24,2432]{1,0:T(8,128)S(1)}, f32[24,2432]{1,0:T(8,128)}, u32[]{:S(2)}) copy-start(f32[24,2432]{1,0:T(8,128)} %get-tuple-element.55) | copy-start | bytes 700420
  144.1 2.8 %copy-start.1 = (f32[24,3,192]{2,0,1:T(8,128)S(1)}, f32[24,3,192]{2,0,1:T(8,128)}, u32[]{:S(2)}) copy-start(f32[24,3,192]{2,0,1:T(8,128)} %param.42) | copy-start | bytes 165892
  144.1 2.8 %copy-start.6 = (f32[24,3,192]{2,0,1:T(8,128)S(1)}, f32[24,3,192]{2,0,1:T(8,128)}, u32[]{:S(2)}) copy-start(f32[24,3,192]{2,0,1:T(8,128)} %param.54) | copy-start | bytes 165892
  144.1 2.8 %copy-start.7 = (f32[24,3,192]{2,0,1:T(8,128)S(1)}, f32[24,3,192]{2,0,1:T(8,128)}, u32[]{:S(2)}) copy-start(f32[24,3,192]{2,0,1:T(8,128)} %param.66) | copy-start | bytes 165892
  144.2 4.2 %copy-start.5 = (f32[192,24]{0,1:T(8,128)S(1)}, f32[192,24]{0,1:T(8,128)}, u32[]{:S(2)}) copy-start(f32[192,24]{0,1:T(8,128)} %param.44) | copy-start | bytes 55300
  144.2 4.2 %copy-start.12 = (f32[192,24]{0,1:T(8,128)S(1)}, f32[192,24]{0,1:T(8,128)}, u32[]{:S(2)}) copy-start(f32[192,24]{0,1:T(8,128)} %param.56) | copy-start | bytes 55300
  144.2 4.2 %copy-start.13 = (f32[192,24]{0,1:T(8,128)S(1)}, f32[192,24]{0,1:T(8,128)}, u32[]{:S(2)}) copy-start(f32[192,24]{0,1:T(8,128)} %param.68) | copy-start | bytes 55300
  144.2 4.8 %copy-start.2 = (f32[24,768]{1,0:T(8,128)S(1)}, f32[24,768]{1,0:T(8,128)}, u32[]{:S(2)}) copy-start(f32[24,768]{1,0:T(8,128)} %up_ref.1) | copy-start | bytes 221188
  144.2 4.8 %copy-start.8 = (f32[24,768]{1,0:T(8,128)S(1)}, f32[24,768]{1,0:T(8,128)}, u32[]{:S(2)}) copy-start(f32[24,768]{1,0:T(8,128)} %param.60) | copy-start | bytes 221188
  144.2 4.8 %copy-start.9 = (f32[24,768]{1,0:T(8,128)S(1)}, f32[24,768]{1,0:T(8,128)}, u32[]{:S(2)}) copy-start(f32[24,768]{1,0:T(8,128)} %param.72) | copy-start | bytes 221188
  144.2 5.9 %copy-start.3 = (f32[768,24]{0,1:T(8,128)S(1)}, f32[768,24]{0,1:T(8,128)}, u32[]{:S(2)}) copy-start(f32[768,24]{0,1:T(8,128)} %param.50) | copy-start | bytes 221188
  144.2 5.9 %copy-start.10 = (f32[768,24]{0,1:T(8,128)S(1)}, f32[768,24]{0,1:T(8,128)}, u32[]{:S(2)}) copy-start(f32[768,24]{0,1:T(8,128)} %param.62) | copy-start | bytes 221188
  144.3 5.8 %copy-start.11 = (f32[768,24]{0,1:T(8,128)S(1)}, f32[768,24]{0,1:T(8,128)}, u32[]{:S(2)}) copy-start(f32[768,24]{0,1:T(8,128)} %param.74) | copy-start | bytes 221188
  146.1 4.7 %copy-start.25 = (f32[24]{0:T(128)S(1)}, f32[24]{0:T(128)}, u32[]{:S(2)}) copy-start(f32[24]{0:T(128)} %param.40) | copy-start | bytes 292
  146.1 4.7 %copy-start.26 = (f32[24]{0:T(128)S(1)}, f32[24]{0:T(128)}, u32[]{:S(2)}) copy-start(f32[24]{0:T(128)} %param.41) | copy-start | bytes 292
  146.1 4.7 %copy-start.33 = (f32[24]{0:T(128)S(1)}, f32[24]{0:T(128)}, u32[]{:S(2)}) copy-start(f32[24]{0:T(128)} %param.53) | copy-start | bytes 292
  146.1 4.8 %copy-start.34 = (f32[24]{0:T(128)S(1)}, f32[24]{0:T(128)}, u32[]{:S(2)}) copy-start(f32[24]{0:T(128)} %param.65) | copy-start | bytes 292
  146.1 4.8 %copy-start.35 = (f32[24]{0:T(128)S(1)}, f32[24]{0:T(128)}, u32[]{:S(2)}) copy-start(f32[24]{0:T(128)} %param.64) | copy-start | bytes 292
  146.1 4.8 %copy-start.36 = (f32[24]{0:T(128)S(1)}, f32[24]{0:T(128)}, u32[]{:S(2)}) copy-start(f32[24]{0:T(128)} %param.52) | copy-start | bytes 292
  146.2 5.3 %copy-start.14 = (f32[2,3,4]{2,0,1:T(2,128)S(1)}, f32[2,3,4]{2,0,1:T(2,128)}, u32[]{:S(2)}) copy-start(f32[2,3,4]{2,0,1:T(2,128)} %param.43) | copy-start | bytes 292
  146.2 5.3 %copy-start.17 = (f32[2,3,4]{2,0,1:T(2,128)S(1)}, f32[2,3,4]{2,0,1:T(2,128)}, u32[]{:S(2)}) copy-start(f32[2,3,4]{2,0,1:T(2,128)} %param.55) | copy-start | bytes 292
  146.2 5.3 %copy-start.18 = (f32[2,3,4]{2,0,1:T(2,128)S(1)}, f32[2,3,4]{2,0,1:T(2,128)}, u32[]{:S(2)}) copy-start(f32[2,3,4]{2,0,1:T(2,128)} %param.67) | copy-start | bytes 292
  146.2 5.9 %copy-start.27 = (f32[24]{0:T(128)S(1)}, f32[24]{0:T(128)}, u32[]{:S(2)}) copy-start(f32[24]{0:T(128)} %param.45) | copy-start | bytes 292
  146.2 5.9 %copy-start.28 = (f32[24]{0:T(128)S(1)}, f32[24]{0:T(128)}, u32[]{:S(2)}) copy-start(f32[24]{0:T(128)} %param.46) | copy-start | bytes 292
  146.2 5.9 %copy-start.37 = (f32[24]{0:T(128)S(1)}, f32[24]{0:T(128)}, u32[]{:S(2)}) copy-start(f32[24]{0:T(128)} %param.58) | copy-start | bytes 292
  146.2 5.9 %copy-start.38 = (f32[24]{0:T(128)S(1)}, f32[24]{0:T(128)}, u32[]{:S(2)}) copy-start(f32[24]{0:T(128)} %param.70) | copy-start | bytes 292
  146.2 5.9 %copy-start.39 = (f32[24]{0:T(128)S(1)}, f32[24]{0:T(128)}, u32[]{:S(2)}) copy-start(f32[24]{0:T(128)} %param.69) | copy-start | bytes 292
  146.3 5.9 %copy-start.40 = (f32[24]{0:T(128)S(1)}, f32[24]{0:T(128)}, u32[]{:S(2)}) copy-start(f32[24]{0:T(128)} %param.57) | copy-start | bytes 292
  146.3 6.4 %copy-start.29 = (f32[24]{0:T(128)S(1)}, f32[24]{0:T(128)}, u32[]{:S(2)}) copy-start(f32[24]{0:T(128)} %param.47) | copy-start | bytes 292
  146.3 6.4 %copy-start.30 = (f32[24]{0:T(128)S(1)}, f32[24]{0:T(128)}, u32[]{:S(2)}) copy-start(f32[24]{0:T(128)} %param.51) | copy-start | bytes 292
  146.3 6.4 %copy-start.41 = (f32[24]{0:T(128)S(1)}, f32[24]{0:T(128)}, u32[]{:S(2)}) copy-start(f32[24]{0:T(128)} %param.63) | copy-start | bytes 292
  146.3 6.4 %copy-start.42 = (f32[24]{0:T(128)S(1)}, f32[24]{0:T(128)}, u32[]{:S(2)}) copy-start(f32[24]{0:T(128)} %param.75) | copy-start | bytes 292
  146.3 6.4 %copy-start.43 = (f32[24]{0:T(128)S(1)}, f32[24]{0:T(128)}, u32[]{:S(2)}) copy-start(f32[24]{0:T(128)} %param.71) | copy-start | bytes 292
  146.3 6.4 %copy-start.44 = (f32[24]{0:T(128)S(1)}, f32[24]{0:T(128)}, u32[]{:S(2)}) copy-start(f32[24]{0:T(128)} %param.59) | copy-start | bytes 292
  146.3 6.9 %copy-start.15 = (f32[12,4]{0,1:T(4,128)S(1)}, f32[12,4]{0,1:T(4,128)}, u32[]{:S(2)}) copy-start(f32[12,4]{0,1:T(4,128)} %param.49) | copy-start | bytes 580
  146.4 6.9 %copy-start.31 = (f32[12,4]{0,1:T(4,128)S(1)}, f32[12,4]{0,1:T(4,128)}, u32[]{:S(2)}) copy-start(f32[12,4]{0,1:T(4,128)} %param.61) | copy-start | bytes 580
  146.4 6.9 %copy-start.32 = (f32[12,4]{0,1:T(4,128)S(1)}, f32[12,4]{0,1:T(4,128)}, u32[]{:S(2)}) copy-start(f32[12,4]{0,1:T(4,128)} %param.73) | copy-start | bytes 580
  146.7 8.3 %copy-start.19 = (f32[24]{0:T(128)}, f32[24]{0:T(128)S(1)}, u32[]{:S(2)}) copy-start(f32[24]{0:T(128)S(1)} %get-tuple-element.206) | copy-start | bytes 292
  146.7 8.3 %copy-start.20 = (f32[24]{0:T(128)}, f32[24]{0:T(128)S(1)}, u32[]{:S(2)}) copy-start(f32[24]{0:T(128)S(1)} %get-tuple-element.207) | copy-start | bytes 292
  146.8 8.3 %copy-start.21 = (f32[24]{0:T(128)}, f32[24]{0:T(128)S(1)}, u32[]{:S(2)}) copy-start(f32[24]{0:T(128)S(1)} %get-tuple-element.208) | copy-start | bytes 292
  146.8 8.3 %copy-start.22 = (f32[24]{0:T(128)}, f32[24]{0:T(128)S(1)}, u32[]{:S(2)}) copy-start(f32[24]{0:T(128)S(1)} %get-tuple-element.209) | copy-start | bytes 292
  146.8 8.3 %copy-start.23 = (f32[24]{0:T(128)}, f32[24]{0:T(128)S(1)}, u32[]{:S(2)}) copy-start(f32[24]{0:T(128)S(1)} %get-tuple-element.211) | copy-start | bytes 292
  146.8 8.3 %copy-start.24 = (f32[24]{0:T(128)}, f32[24]{0:T(128)S(1)}, u32[]{:S(2)}) copy-start(f32[24]{0:T(128)S(1)} %get-tuple-element.212) | copy-start | bytes 292
  150.1 5.0 %copy-start.16 = (f32[12,4]{0,1:T(4,128)}, f32[12,4]{0,1:T(4,128)S(1)}, u32[]{:S(2)}) copy-start(f32[12,4]{0,1:T(4,128)S(1)} %copy.145) | copy-start | bytes 580
